TPU v7x, 32 devices: a whole 2x2x4 slice. The times are simulated.
32 devices in a mesh: outer: 4 (over y, x), inner: 8 (over z, core).
Axes of the slice: x: 2, y: 2, z: 4, core: 2. Of those that a mesh axis runs over, the one named last changes fastest.
Arguments:
- activations: bfloat16 [4096, 128], P(('outer', 'inner')), may hold values from -6 to 6
- out_grads: bfloat16 [4096, 8192], P(('outer', 'inner')), may hold values from -6 to 6
- momentum: float32 [8192, 128], P(('outer', 'inner')), may hold values from -6 to 6
- first_exp: int32 [8192], replicated, may hold values from -3 to -1
- second_exp: int32 [8192], replicated, may hold values from -2 to 2
- third_exp: int32 [8192], replicated, may hold values from -7 to -5
- signs: int32 [2, 128], replicated, may hold values from 0 to 1
Outputs:
- new_momentum: float32 [8192, 128], P(('outer', 'inner'))
- update: bfloat16 [128, 8192], replicated
All inputs are finite; a program needn't handle non-finite values.
Results may differ from a plain program's by a relative error of at most 0.017.
Values may be sent and summed in bfloat16 or wider, within the bound.
No kernel may reach another device: no remote copies, remote signals or barrier semaphores. Data moves between devices by JAX's collectives and lax.ppermute only.
A program may use at most 64 MiB of HBM per device.

v0:
```python
import jax
import jax.numpy as jnp
from jax import lax
from jax.experimental import pallas as pl
from jax.experimental.pallas import tpu as pltpu
from jax.sharding import PartitionSpec as P


quant_limit = 127.0
momentum_decay = 0.9
step_size = 0.5


def hadamard_matrix(order):
    position = jnp.arange(order, dtype=jnp.int32)
    common = jnp.bitwise_and(position[:, None], position[None, :])
    parity = jnp.zeros((order, order), jnp.int32)
    for shift_by in range(order.bit_length() - 1):
        parity = parity + jnp.bitwise_and(jnp.right_shift(common, shift_by), 1)
    return 1.0 - 2.0 * jnp.bitwise_and(parity, 1).astype(jnp.float32)


def rotation(sign_bits):
    order = sign_bits.shape[0]
    flips = 1.0 - 2.0 * sign_bits.astype(jnp.float32)
    return flips[:, None] * hadamard_matrix(order) / jnp.sqrt(jnp.float32(order))


def collect(pieces):
    grouped = lax.all_gather(pieces[None], "outer", axis=0, tiled=True)
    spread = lax.all_gather(grouped, "inner", axis=1, tiled=True)
    return spread.reshape(-1, pieces.shape[1])


def general(activations, out_grads, momentum, first_exp, second_exp, third_exp, signs):
    high = lax.Precision.HIGHEST
    outer_count = lax.axis_size("outer")
    inner_count = lax.axis_size("inner")
    outer_place = lax.axis_index("outer")
    inner_place = lax.axis_index("inner")
    device_count = outer_count * inner_count
    first_rot = rotation(signs[0])
    second_rot = rotation(signs[1])
    grad = lax.dot_general(
        activations, out_grads, (((0,), (0,)), ((), ())), preferred_element_type=jnp.float32
    )
    slab_shape = grad.shape
    order = first_rot.shape[0]
    count_blocks = grad.size // order
    shard_rows = count_blocks // device_count
    rotated = jnp.dot(grad.reshape(count_blocks, order), first_rot, precision=high)
    first_down = jnp.exp2(-first_exp.astype(jnp.float32))[:, None]
    quant_first = jnp.clip(rotated * first_down, -quant_limit, quant_limit).astype(jnp.bfloat16)
    grouped = quant_first.astype(jnp.float32).reshape(outer_count, inner_count * shard_rows, order)
    inner_total = lax.psum_scatter(
        grouped.astype(jnp.bfloat16), "inner", scatter_dimension=1, tiled=True
    ).astype(jnp.float32)
    first_grid = first_exp.reshape(outer_count, inner_count, shard_rows)
    second_grid = second_exp.reshape(outer_count, inner_count, shard_rows)
    third_grid = third_exp.reshape(outer_count, inner_count, shard_rows)
    first_here = lax.dynamic_index_in_dim(first_grid, inner_place, 1, keepdims=False)
    second_here = lax.dynamic_index_in_dim(second_grid, inner_place, 1, keepdims=False)
    shift_scale = jnp.exp2((first_here - second_here).astype(jnp.float32))[:, :, None]
    requant = jnp.clip(inner_total * shift_scale, -quant_limit, quant_limit).astype(jnp.bfloat16)
    total = lax.psum_scatter(
        requant.astype(jnp.float32).astype(jnp.bfloat16), "outer", scatter_dimension=0, tiled=True
    ).astype(jnp.float32)[0]
    second_mine = lax.dynamic_index_in_dim(second_here, outer_place, 0, keepdims=False)
    second_up = jnp.exp2(second_mine.astype(jnp.float32))[:, None]
    mean_grad = jnp.dot(total * second_up, first_rot.T, precision=high) / device_count
    new_momentum = momentum_decay * momentum + mean_grad
    third_row = lax.dynamic_index_in_dim(third_grid, outer_place, 0, keepdims=False)
    third_mine = lax.dynamic_index_in_dim(third_row, inner_place, 0, keepdims=False)
    rotated_step = jnp.dot(-step_size * new_momentum, second_rot, precision=high)
    third_down = jnp.exp2(-third_mine.astype(jnp.float32))[:, None]
    quant_third = jnp.clip(rotated_step * third_down, -quant_limit, quant_limit).astype(
        jnp.bfloat16
    )
    third_up = jnp.exp2(third_mine.astype(jnp.float32))[:, None]
    restored = jnp.dot(quant_third.astype(jnp.float32) * third_up, second_rot.T, precision=high)
    update = collect(restored.astype(jnp.bfloat16)).reshape(slab_shape)
    return (new_momentum, update)


def vmem(mebibytes):
    return pltpu.CompilerParams(vmem_limit_bytes=mebibytes * 1024 * 1024)


def log2(count):
    return count.bit_length() - 1


def tile(count, most):
    return min(count & -count, most)


def power_of_two(count):
    return count > 0 and count & (count - 1) == 0


class Plan:
    def __init__(self, activations, out_grads, signs, outer, inner):
        self.outer, self.inner = outer, inner
        self.levels = inner // 2
        self.tokens, self.rows = activations.shape
        self.order = signs.shape[1]
        self.width = out_grads.shape[1]
        self.chunks = self.width // self.order
        self.own_rows = self.rows // (outer * inner)
        self.seg_rows = outer * self.own_rows
        self.slab_rows = self.levels * self.own_rows

    def fits(self):
        return (
            all(power_of_two(n) for n in (self.outer, self.inner, self.rows, self.chunks))
            and self.levels == 4
            and self.own_rows * self.outer * self.inner == self.rows
            and self.seg_rows == 16
            and self.slab_rows == 16
            and self.order == 128
            and 2 * self.chunks == self.order
        )


def places():
    outer_place = lax.axis_index("outer")
    inner_place = lax.axis_index("inner")
    return outer_place, inner_place >> 1, inner_place & 1


def iota(shape, axis):
    return lax.broadcasted_iota(jnp.int32, shape, axis)


def pick(plan, row_of, scale):
    count = row_of.shape[0]
    lines = scale.shape[0]
    line = iota((count, lines), 1)
    row_of = jnp.broadcast_to(row_of, (count, lines))
    even = jnp.where(row_of == 2 * line, 1.0, 0.0).astype(jnp.bfloat16)
    odd = jnp.where(row_of == 2 * line + 1, 1.0, 0.0).astype(jnp.bfloat16)
    table = scale.astype(jnp.bfloat16)
    half = plan.chunks
    low = jnp.dot(even, table[:, :half], preferred_element_type=jnp.float32)
    high = jnp.dot(odd, table[:, half:], preferred_element_type=jnp.float32)
    return low + high


def two_terms(values):
    high = values.astype(jnp.bfloat16)
    low = (values - high.astype(jnp.float32)).astype(jnp.bfloat16)
    return jnp.concatenate([high, low], axis=1)


def clip_round(values):
    return jnp.clip(values, -quant_limit, quant_limit).astype(jnp.bfloat16)


def turn_matrix(order):
    bits = iota((order, order), 0) & iota((order, order), 1)
    for shift_by in (4, 2, 1):
        bits = bits ^ (bits >> shift_by)
    return (1 - 2 * (bits & 1)).astype(jnp.float32).astype(jnp.bfloat16)


def front(plan, span, mine, activations, out_grads, first_exp, signs):
    first_chunk, chunk_count = span
    group = tile(chunk_count, 8)
    groups = chunk_count // group
    half_rows = plan.rows // 2
    seg = plan.seg_rows
    wide = group * plan.order

    def kernel(acts_hbm, grads_hbm, exp_hbm, signs_hbm, *refs):
        out, (acts_ref, grads_ref, exp_ref, signs_ref, sems) = refs[0], refs[1:]
        copies = [
            pltpu.make_async_copy(signs_hbm, signs_ref, sems.at[0]),
            pltpu.make_async_copy(acts_hbm, acts_ref, sems.at[1]),
            pltpu.make_async_copy(exp_hbm, exp_ref, sems.at[2]),
        ]
        for step in range(groups):
            at = (first_chunk + step * group) * plan.order
            copies.append(
                pltpu.make_async_copy(
                    grads_hbm.at[:, pl.ds(at, wide)], grads_ref.at[step], sems.at[3 + step]
                )
            )
        for copy in copies:
            copy.start()
        outer_place, level, core = places()
        keeper = core if mine else 1 - core
        index = iota((half_rows, 1), 0)
        own = index & (plan.own_rows - 1)
        hop_outer = (index >> log2(plan.own_rows)) & (plan.outer - 1)
        hop_level = index >> log2(seg)
        inner_of = 2 * (level ^ hop_level) + keeper
        row_of = ((outer_place ^ hop_outer) * plan.inner + inner_of) * plan.own_rows + own
        chooser = jnp.where(
            iota((half_rows, plan.rows), 1) == jnp.broadcast_to(row_of, (half_rows, plan.rows)),
            1.0,
            0.0,
        ).astype(jnp.bfloat16)
        root = 1.0 / (plan.order**0.5)
        square = (plan.order, plan.order)
        hadamard = turn_matrix(plan.order)
        for copy in copies:
            copy.wait()
        flips = 1.0 - 2.0 * signs_ref[0:1, :].astype(jnp.float32)
        diagonal = jnp.where(iota(square, 0) == iota(square, 1), flips, 0.0).astype(jnp.bfloat16)
        turn = jnp.dot(diagonal, hadamard, preferred_element_type=jnp.float32).astype(jnp.bfloat16)
        turn = jnp.concatenate([turn, turn], axis=0)
        acts = lax.dot_general(
            chooser, acts_ref[...], (((1,), (1,)), ((), ())), preferred_element_type=jnp.float32
        ).astype(jnp.bfloat16)
        down = pick(plan, row_of, jnp.exp2(-exp_ref[...].astype(jnp.float32))) * root
        for step in range(groups):
            grad = jnp.dot(acts, grads_ref[step], preferred_element_type=jnp.float32)
            stacked = jnp.concatenate(
                [grad[:, c * plan.order : (c + 1) * plan.order] for c in range(group)], axis=0
            )
            rotated = jnp.dot(two_terms(stacked), turn, preferred_element_type=jnp.float32)
            for c in range(group):
                at = first_chunk + step * group + c
                part = rotated[c * half_rows : (c + 1) * half_rows] * down[:, at : at + 1]
                part = clip_round(part)
                for hop in range(plan.levels):
                    row = (hop * chunk_count + step * group + c) * seg
                    out[pl.ds(row, seg), :] = part[hop * seg : (hop + 1) * seg]

    return pl.pallas_call(
        kernel,
        out_shape=jax.ShapeDtypeStruct(
            (plan.levels * chunk_count * seg, plan.order), jnp.bfloat16
        ),
        in_specs=[pl.BlockSpec(memory_space=pltpu.HBM)] * 4,
        out_specs=pl.BlockSpec(memory_space=pltpu.VMEM),
        scratch_shapes=[
            pltpu.VMEM(activations.shape, jnp.bfloat16),
            pltpu.VMEM((groups, plan.tokens, wide), jnp.bfloat16),
            pltpu.VMEM(first_exp.shape, jnp.int32),
            pltpu.VMEM(signs.shape, jnp.int32),
            pltpu.SemaphoreType.DMA((groups + 3,)),
        ],
        compiler_params=vmem(16 if mine or first_chunk else 60),
        name="front_mine" if mine else "front_theirs",
    )(activations, out_grads, first_exp, signs)


def join_cores(plan, ours, theirs):
    rows = ours.shape[0] // plan.levels

    def kernel(one, two, *outs):
        for hop, out in enumerate(outs):
            at = pl.ds(hop * rows, rows)
            total = one[at, :].astype(jnp.float32) + two[at, :].astype(jnp.float32)
            out[...] = total.astype(jnp.bfloat16)

    piece = jax.ShapeDtypeStruct((rows, ours.shape[1]), jnp.bfloat16)
    return pl.pallas_call(
        kernel, out_shape=[piece] * plan.levels, compiler_params=vmem(16), name="join_cores"
    )(ours, theirs)


def requantize(plan, spans, first_exp, second_exp, parts):
    first_chunk, chunk_count = whole_span(spans)
    seg = plan.seg_rows
    levels = plan.levels

    def kernel(first_ref, second_ref, *refs):
        ins, outs = refs[: levels * len(spans)], refs[levels * len(spans) :]
        outer_place, level, core = places()
        index = iota((seg, 1), 0)
        own = index & (plan.own_rows - 1)
        hop = index >> log2(plan.own_rows)
        inner_of = 2 * level + core
        row_of = ((outer_place ^ hop) * plan.inner + inner_of) * plan.own_rows + own
        shift = pick(plan, row_of, jnp.exp2((first_ref[...] - second_ref[...]).astype(jnp.float32)))
        for n, (span_chunk, span_count) in enumerate(spans):
            group = tile(span_count, 16)
            size = group * seg
            here, there = iota((size, size), 0), iota((size, size), 1)
            source = (here & (group - 1)) * seg + (here >> log2(group))
            order = jnp.where(there == source, 1.0, 0.0).astype(jnp.bfloat16)
            for step in range(span_count // group):
                rows = pl.ds(step * size, size)
                total = ins[n * levels][rows, :].astype(jnp.float32)
                for other in ins[n * levels + 1 : (n + 1) * levels]:
                    total = total + other[rows, :].astype(jnp.float32)
                start = span_chunk + step * group
                scaled = jnp.concatenate(
                    [
                        total[c * seg : (c + 1) * seg] * shift[:, start + c : start + c + 1]
                        for c in range(group)
                    ],
                    axis=0,
                )
                moved = jnp.dot(order, clip_round(scaled), preferred_element_type=jnp.float32)
                moved = moved.astype(jnp.bfloat16)
                for m in range(seg):
                    row = (m % plan.own_rows) * chunk_count + start - first_chunk
                    outs[m // plan.own_rows][pl.ds(row, group), :] = moved[
                        m * group : (m + 1) * group
                    ]

    piece = jax.ShapeDtypeStruct((plan.own_rows * chunk_count, plan.order), jnp.bfloat16)
    return pl.pallas_call(
        kernel, out_shape=[piece] * plan.outer, compiler_params=vmem(12), name="requantize"
    )(first_exp, second_exp, *[piece for span_parts in parts for piece in span_parts])


def whole_span(spans):
    return (spans[0][0], sum(count for start, count in spans))


def owner(plan, span, second_exp, third_exp, signs, momentum, parts):
    first_chunk, chunk_count = span
    own_rows, order = plan.own_rows, plan.order
    devices = plan.outer * plan.inner

    def kernel(second_ref, third_ref, signs_ref, momentum_ref, *refs):
        ins, (moment_out, update_out) = refs[: plan.outer], refs[plan.outer :]
        outer_place, level, core = places()
        first_row = (outer_place * plan.inner + 2 * level + core) * own_rows
        row_of = first_row + iota((own_rows, 1), 0)
        diagonal = iota((chunk_count, chunk_count), 0) == iota((chunk_count, chunk_count), 1)

        def column(table):
            chosen = pick(plan, row_of, table)[:, first_chunk : first_chunk + chunk_count]
            return jnp.concatenate(
                [
                    jnp.sum(jnp.where(diagonal, chosen[k : k + 1], 0.0), axis=1, keepdims=True)
                    for k in range(own_rows)
                ],
                axis=0,
            )

        second = second_ref[...].astype(jnp.float32)
        third = third_ref[...].astype(jnp.float32)
        up, third_down, third_up = (column(jnp.exp2(e)) for e in (second, -third, third))
        root = 1.0 / (order**0.5)
        total = ins[0][...].astype(jnp.float32)
        for other in ins[1:]:
            total = total + other[...].astype(jnp.float32)
        flips = 1.0 - 2.0 * signs_ref[...].astype(jnp.float32)
        one, two = flips[0:1, :], flips[1:2, :]
        turn = turn_matrix(order)
        twice = jnp.concatenate([turn, turn], axis=0)
        back = jnp.dot(two_terms(total * up), twice, preferred_element_type=jnp.float32)
        before = jnp.concatenate(
            [
                momentum_ref[pl.ds(k * plan.chunks + first_chunk, chunk_count), :]
                for k in range(own_rows)
            ],
            axis=0,
        )
        moment = momentum_decay * before + back * (one * (root / devices))
        moment_out[...] = moment
        turned = jnp.dot(
            two_terms(moment * (-step_size * two)), twice, preferred_element_type=jnp.float32
        )
        quant = clip_round(turned * (third_down * root))
        restored = jnp.dot(quant, turn, preferred_element_type=jnp.float32)
        update_out[...] = (restored * (third_up * root) * two).astype(jnp.bfloat16)

    shape = (own_rows * chunk_count, order)
    return pl.pallas_call(
        kernel,
        out_shape=[
            jax.ShapeDtypeStruct(shape, jnp.float32),
            jax.ShapeDtypeStruct(shape, jnp.bfloat16),
        ],
        compiler_params=vmem(8),
        name="owner",
    )(second_exp, third_exp, signs, momentum, *parts)


def band_of(level, core):
    return core ^ (level >> 1)


def half_slab(plan, span, pair, near, far):
    _, chunk_count = span
    own_rows, rows = plan.own_rows, plan.slab_rows
    group = tile(chunk_count, 16)
    size = group * rows

    def kernel(pair_ref, near_ref, far_ref, out):
        _, level, core = places()
        here, there = iota((size, size), 0), iota((size, size), 1)
        row = here & (rows - 1)
        device = row >> log2(own_rows)
        side = ((device >> 1) ^ level) & 1
        part = 2 * side + ((device ^ core) & 1)
        source = (part * own_rows + (row & (own_rows - 1))) * group + (here >> log2(rows))
        order = jnp.where(there == source, 1.0, 0.0).astype(jnp.bfloat16)
        lower = core == 0
        for step in range(chunk_count // group):
            blocks = []
            for one, two in ((pair_ref, near_ref), (near_ref, far_ref)):
                for k in range(2 * own_rows):
                    at = pl.ds(k * chunk_count + step * group, group)
                    blocks.append(jnp.where(lower, one[at, :], two[at, :]))
            block = jnp.concatenate(blocks, axis=0)
            moved = jnp.dot(order, block, preferred_element_type=jnp.float32).astype(jnp.bfloat16)
            for c in range(group):
                at = (step * group + c) * plan.order
                out[:, pl.ds(at, plan.order)] = moved[c * rows : (c + 1) * rows]

    shape = jax.ShapeDtypeStruct((rows, chunk_count * plan.order), jnp.bfloat16)
    return pl.pallas_call(
        kernel, out_shape=shape, compiler_params=vmem(8), name="half_slab"
    )(pair, near, far)


def place_slabs(plan, ours, theirs):
    spans = plan.spans

    def kernel(*refs):
        (out, sems), ins = refs[-2:], refs[:-2]
        outer_place, level, core = places()
        copies = []
        for n, (first_chunk, chunk_count) in enumerate(spans):
            for side in range(2):
                band = band_of(level, core) if side == 0 else 1 - band_of(level, core)
                for hop in range(plan.outer):
                    at = (n * 2 + side) * plan.outer + hop
                    row = ((outer_place ^ hop) * 2 + band) * plan.slab_rows
                    copies.append(
                        pltpu.make_async_copy(
                            ins[at],
                            out.at[
                                pl.ds(row, plan.slab_rows),
                                pl.ds(first_chunk * plan.order, chunk_count * plan.order),
                            ],
                            sems.at[at],
                        )
                    )
        for copy in copies:
            copy.start()
        for copy in copies:
            copy.wait()

    flat = [piece for n in range(len(spans)) for side in (ours[n], theirs[n]) for piece in side]
    return pl.pallas_call(
        kernel,
        out_shape=jax.ShapeDtypeStruct((plan.rows, plan.width), jnp.bfloat16),
        in_specs=[pl.BlockSpec(memory_space=pl.ANY)] * len(flat),
        out_specs=pl.BlockSpec(memory_space=pl.ANY),
        scratch_shapes=[pltpu.SemaphoreType.DMA((len(flat),))],
        compiler_params=vmem(8),
        name="place_slabs",
    )(*flat)


def send(plan, value, target_of):
    pairs = []
    for o in range(plan.outer):
        for z in range(plan.levels):
            for c in range(2):
                target = target_of(o, z, c)
                if target is not None:
                    to, tz, tc = target
                    pairs.append((o * plan.inner + 2 * z + c, to * plan.inner + 2 * tz + tc))
    return lax.ppermute(value, ("outer", "inner"), pairs)


def swap_cores(plan, value):
    return send(plan, value, lambda o, z, c: (o, z, 1 - c))


def over_levels(plan, value, hop):
    return send(plan, value, lambda o, z, c: (o, z ^ hop, c))


def over_outer(plan, value, hop):
    return send(plan, value, lambda o, z, c: (o ^ hop, z, c))


def to_near(plan, value):
    return send(plan, value, lambda o, z, c: (o, z ^ (2 if c else 1), c))


def to_far(plan, value):
    return send(plan, value, lambda o, z, c: (o, z ^ 3, c) if c else None)


def stream_front(plan, span, activations, out_grads, first_exp, signs):
    theirs = front(plan, span, False, activations, out_grads, first_exp, signs)
    theirs = swap_cores(plan, theirs)
    ours = front(plan, span, True, activations, out_grads, first_exp, signs)
    joined = join_cores(plan, ours, theirs)
    parts = [joined[0]]
    for hop in range(1, plan.levels):
        parts.append(over_levels(plan, joined[hop], hop))
    return parts


def stream_back(plan, spans, tables, momentum, parts):
    first_exp, second_exp, third_exp, signs = tables
    span = whole_span(spans)
    parts = requantize(plan, spans, first_exp, second_exp, parts)
    pieces = [parts[0]]
    for hop in range(1, plan.outer):
        pieces.append(over_outer(plan, parts[hop], hop))
    moment, update = owner(plan, span, second_exp, third_exp, signs, momentum, pieces)
    pair = jnp.concatenate([update, swap_cores(plan, update)], axis=0)
    near = to_near(plan, pair)
    far = to_far(plan, pair)
    slab = half_slab(plan, span, pair, near, far)
    ours = [slab]
    for hop in range(1, plan.outer):
        ours.append(over_outer(plan, slab, hop))
    theirs = []
    for hop in range(plan.outer):
        theirs.append(swap_cores(plan, ours[hop]))
    return moment, ours, theirs


def on_device(activations, out_grads, momentum, first_exp, second_exp, third_exp, signs):
    plan = Plan(activations, out_grads, signs, lax.axis_size("outer"), lax.axis_size("inner"))
    if not plan.fits():
        return general(activations, out_grads, momentum, first_exp, second_exp, third_exp, signs)
    exps = [e.reshape(-1, plan.order) for e in (first_exp, second_exp, third_exp)]
    groups = split_chunks(plan.chunks)
    plan.spans = [whole_span(spans) for spans in groups]
    fronts = {}
    for spans in groups:
        for span in spans:
            fronts[span] = stream_front(plan, span, activations, out_grads, exps[0], signs)
    done = [
        stream_back(plan, spans, (*exps, signs), momentum, [fronts[span] for span in spans])
        for spans in groups
    ]
    moments = [d[0].reshape(plan.own_rows, -1, plan.order) for d in done]
    new_momentum = jnp.concatenate(moments, axis=1).reshape(momentum.shape)
    update = place_slabs(plan, [d[1] for d in done], [d[2] for d in done])
    return (new_momentum, update)


def split_chunks(chunks):
    half = chunks // 2
    return [[(0, half), (half, chunks - half)]]


def solution(mesh):
    in_specs = (
        P(("outer", "inner"), None),
        P(("outer", "inner"), None),
        P(("outer", "inner"), None),
        P(),
        P(),
        P(),
        P(),
    )
    out_specs = (P(("outer", "inner"), None), P())
    return jax.shard_map(
        on_device, mesh=mesh, in_specs=in_specs, out_specs=out_specs, check_vma=False
    )
```

profile of v0, /device:TPU:0, one launch (start us, length us, event | category | flops | bytes accessed | tf_op | source)
XLA Modules:
  0.0 71.5 jit_solution(14281486373140396204)
XLA Ops:
  0.6 0.0 copy-start.6
  0.6 0.0 copy-start
  0.7 0.0 copy-start.2
  0.7 0.0 copy-start.1
  0.7 3.1 %front_theirs.2 = bf16[2048,128]{1,0:T(8,128)(2,1)} custom-call(bf16[128,128]{1,0:T(8,128)(2,1)} %acts_hbm.7, bf16[128,8192]{1,0:T(8,128)(2,1)} %grads_hbm.7, s32[64,128]{1,0:T(8,128)} %bitcast.3, s32[2,128]{1,0:T(2,128)} %signs_ref.1), custom_call_target="tpu_custom_call" | custom-call | tf_op jit(solution)/shard_map/front_theirs/pallas_call | solution.py:230
  3.8 0.6 collective-permute-start
  4.3 0.0 copy-done.6
  4.3 0.0 copy-done
  4.3 0.0 copy-done.2
  4.3 0.0 copy-done.1
  4.4 1.1 %front_theirs.3 = bf16[2048,128]{1,0:T(8,128)(2,1)S(1)} custom-call(bf16[128,128]{1,0:T(8,128)(2,1)S(1)} %copy-done.2, bf16[128,8192]{1,0:T(8,128)(2,1)S(1)} %copy-done, s32[64,128]{1,0:T(8,128)S(1)} %bitcast.4, s32[2,128]{1,0:T(2,128)S(1)} %copy-done.6), custom_call_target="tpu_custom_call" | custom-call | tf_op jit(solution)/shard_map/front_theirs/pallas_call | solution.py:230
  5.5 0.1 collective-permute-start.4
  5.6 1.1 %front_mine.2.one = bf16[2048,128]{1,0:T(8,128)(2,1)S(1)} custom-call(bf16[128,128]{1,0:T(8,128)(2,1)S(1)} %copy-done.2, bf16[128,8192]{1,0:T(8,128)(2,1)S(1)} %copy-done, s32[64,128]{1,0:T(8,128)S(1)} %bitcast.5, s32[2,128]{1,0:T(2,128)S(1)} %copy-done.6), custom_call_target="tpu_custom_call" | custom-call | tf_op jit(solution)/shard_map/front_mine/pallas_call | solution.py:230
  6.7 0.0 collective-permute-done.two
  6.7 0.1 join_cores.2
  6.9 0.0 copy-start.3
  6.9 0.0 copy-start.4
  6.9 0.0 copy-start.5
  6.9 3.1 %collective-permute-start.1 = (bf16[512,128]{1,0:T(8,128)(2,1)S(1)}, bf16[512,128]{1,0:T(8,128)(2,1)S(1)}, u32[]{:S(2)}, u32[]{:S(2)}) collective-permute-start(bf16[512,128]{1,0:T(8,128)(2,1)S(1)} %get-tuple-element.17), channel_id=1, source_target_pairs={{0,2},{1,3},{2,0},{3,1},{4,6},{5,7},{6,4},{7,5},{8,10},{9,11},{10,... | collective-permute-start | bytes 393224 | tf_op jit(solution)/shard_map/ppermute | solution.py:464
  10.0 1.1 %front_mine.3.one = bf16[2048,128]{1,0:T(8,128)(2,1)S(1)} custom-call(bf16[128,128]{1,0:T(8,128)(2,1)S(1)} %copy-done.2, bf16[128,8192]{1,0:T(8,128)(2,1)S(1)} %copy-done, s32[64,128]{1,0:T(8,128)S(1)} %bitcast.6, s32[2,128]{1,0:T(2,128)S(1)} %copy-done.6), custom_call_target="tpu_custom_call" | custom-call | tf_op jit(solution)/shard_map/front_mine/pallas_call | solution.py:230
  11.1 2.7 %collective-permute-start.2 = (bf16[512,128]{1,0:T(8,128)(2,1)S(1)}, bf16[512,128]{1,0:T(8,128)(2,1)S(1)}, u32[]{:S(2)}, u32[]{:S(2)}) collective-permute-start(bf16[512,128]{1,0:T(8,128)(2,1)S(1)} %get-tuple-element.18), channel_id=1, source_target_pairs={{0,4},{1,5},{2,6},{3,7},{4,0},{5,1},{6,2},{7,3},{8,12},{9,13},{10,... | collective-permute-start | bytes 393224 | tf_op jit(solution)/shard_map/ppermute | solution.py:464
  13.8 0.0 collective-permute-start.3
  13.8 0.0 collective-permute-done.4.two
  13.8 0.1 join_cores.3
  13.9 1.0 %collective-permute-start.5 = (bf16[512,128]{1,0:T(8,128)(2,1)S(1)}, bf16[512,128]{1,0:T(8,128)(2,1)S(1)}, u32[]{:S(2)}, u32[]{:S(2)}) collective-permute-start(bf16[512,128]{1,0:T(8,128)(2,1)S(1)} %get-tuple-element.21), channel_id=1, source_target_pairs={{0,2},{1,3},{2,0},{3,1},{4,6},{5,7},{6,4},{7,5},{8,10},{9,11},{10,... | collective-permute-start | bytes 393224 | tf_op jit(solution)/shard_map/ppermute | solution.py:464
  14.9 3.5 %collective-permute-start.6 = (bf16[512,128]{1,0:T(8,128)(2,1)S(1)}, bf16[512,128]{1,0:T(8,128)(2,1)S(1)}, u32[]{:S(2)}, u32[]{:S(2)}) collective-permute-start(bf16[512,128]{1,0:T(8,128)(2,1)S(1)} %get-tuple-element.22), channel_id=1, source_target_pairs={{0,4},{1,5},{2,6},{3,7},{4,0},{5,1},{6,2},{7,3},{8,12},{9,13},{10,... | collective-permute-start | bytes 393224 | tf_op jit(solution)/shard_map/ppermute | solution.py:464
  18.4 0.0 collective-permute-done.1.refs_1_
  18.4 0.2 collective-permute-start.7
  18.6 5.6 %collective-permute-done.2.refs_2_ = bf16[512,128]{1,0:T(8,128)(2,1)S(1)} collective-permute-done((bf16[512,128]{1,0:T(8,128)(2,1)S(1)}, bf16[512,128]{1,0:T(8,128)(2,1)S(1)}, u32[]{:S(2)}, u32[]{:S(2)}) %collective-permute-start.2) | collective-permute-done | bytes 131104 | tf_op jit(solution)/shard_map/ppermute | solution.py:464
  24.1 0.0 collective-permute-done.3.refs_3_
  24.1 0.0 collective-permute-done.5.refs_5_
  24.1 10.9 %collective-permute-done.6.refs_6_ = bf16[512,128]{1,0:T(8,128)(2,1)S(1)} collective-permute-done((bf16[512,128]{1,0:T(8,128)(2,1)S(1)}, bf16[512,128]{1,0:T(8,128)(2,1)S(1)}, u32[]{:S(2)}, u32[]{:S(2)}) %collective-permute-start.6) | collective-permute-done | bytes 131104 | tf_op jit(solution)/shard_map/ppermute | solution.py:464
  35.0 0.0 collective-permute-done.7.refs_7_
  35.0 0.0 copy-done.3
  35.0 0.7 %requantize.1 = (bf16[256,128]{1,0:T(8,128)(2,1)S(1)}, bf16[256,128]{1,0:T(8,128)(2,1)S(1)}, bf16[256,128]{1,0:T(8,128)(2,1)S(1)}, bf16[256,128]{1,0:T(8,128)(2,1)S(1)}) custom-call(s32[64,128]{1,0:T(8,128)S(1)} %bitcast.7, s32[64,128]{1,0:T(8,128)S(1)} %bitcast.8, bf16[512,128]{1,0:T(8,128)(2,1)S(1)} %get-tuple-element.16.refs_0_, ...), custom_call_target="tpu_custom_call" | custom-call | tf_op jit(solution)/shard_map/requantize/pallas_call | solution.py:306
  35.8 1.5 %collective-permute-start.8 = (bf16[256,128]{1,0:T(8,128)(2,1)S(1)}, bf16[256,128]{1,0:T(8,128)(2,1)S(1)}, u32[]{:S(2)}, u32[]{:S(2)}) collective-permute-start(bf16[256,128]{1,0:T(8,128)(2,1)S(1)} %get-tuple-element.25), channel_id=1, source_target_pairs={{0,8},{1,9},{2,10},{3,11},{4,12},{5,13},{6,14},{7,15},{8,0},{9,1},... | collective-permute-start | bytes 196616 | tf_op jit(solution)/shard_map/ppermute | solution.py:464
  37.3 1.5 %collective-permute-start.9 = (bf16[256,128]{1,0:T(8,128)(2,1)S(1)}, bf16[256,128]{1,0:T(8,128)(2,1)S(1)}, u32[]{:S(2)}, u32[]{:S(2)}) collective-permute-start(bf16[256,128]{1,0:T(8,128)(2,1)S(1)} %get-tuple-element.26), channel_id=1, source_target_pairs={{0,16},{1,17},{2,18},{3,19},{4,20},{5,21},{6,22},{7,23},{8,24},{9,... | collective-permute-start | bytes 196616 | tf_op jit(solution)/shard_map/ppermute | solution.py:464
  38.8 0.5 collective-permute-start.10
  39.3 1.3 %collective-permute-done.8.refs_1_ = bf16[256,128]{1,0:T(8,128)(2,1)S(1)} collective-permute-done((bf16[256,128]{1,0:T(8,128)(2,1)S(1)}, bf16[256,128]{1,0:T(8,128)(2,1)S(1)}, u32[]{:S(2)}, u32[]{:S(2)}) %collective-permute-start.8) | collective-permute-done | bytes 65568 | tf_op jit(solution)/shard_map/ppermute | solution.py:464
  40.6 1.2 %collective-permute-done.9.refs_2_ = bf16[256,128]{1,0:T(8,128)(2,1)S(1)} collective-permute-done((bf16[256,128]{1,0:T(8,128)(2,1)S(1)}, bf16[256,128]{1,0:T(8,128)(2,1)S(1)}, u32[]{:S(2)}, u32[]{:S(2)}) %collective-permute-start.9) | collective-permute-done | bytes 65568 | tf_op jit(solution)/shard_map/ppermute | solution.py:464
  41.8 2.2 %collective-permute-done.10.refs_3_ = bf16[256,128]{1,0:T(8,128)(2,1)S(1)} collective-permute-done((bf16[256,128]{1,0:T(8,128)(2,1)S(1)}, bf16[256,128]{1,0:T(8,128)(2,1)S(1)}, u32[]{:S(2)}, u32[]{:S(2)}) %collective-permute-start.10) | collective-permute-done | bytes 65568 | tf_op jit(solution)/shard_map/ppermute | solution.py:464
  44.0 1.2 %owner.1 = (f32[256,128]{1,0:T(8,128)}, bf16[256,128]{1,0:T(8,128)(2,1)S(1)}) custom-call(s32[64,128]{1,0:T(8,128)S(1)} %bitcast.9, s32[64,128]{1,0:T(8,128)S(1)} %bitcast.10, s32[2,128]{1,0:T(2,128)S(1)} %copy-done.6, f32[256,128]{1,0:T(8,128)S(1)} %copy-done.4, bf16[256,128]{1,0:T(8,128)(2,1)S(1)} %get-tuple-element.24.refs_0_, ...), custom_call_target="tpu_custom_call" | custom-call | tf_op jit(solution)/shard_map/owner/pallas_call | solution.py:366
  45.2 0.0 collective-permute-start.11
  45.3 1.2 %collective-permute-done.11 = bf16[256,128]{1,0:T(8,128)(2,1)S(1)} collective-permute-done((bf16[256,128]{1,0:T(8,128)(2,1)S(1)}, bf16[256,128]{1,0:T(8,128)(2,1)S(1)}, u32[]{:S(2)}, u32[]{:S(2)}) %collective-permute-start.11) | collective-permute-done | bytes 65568 | tf_op jit(solution)/shard_map/ppermute | solution.py:464
  46.5 0.7 collective-permute-start.13
  47.2 2.6 %collective-permute-start.12 = (bf16[512,128]{1,0:T(8,128)(2,1)S(1)}, bf16[512,128]{1,0:T(8,128)(2,1)S(1)}, u32[]{:S(2)}, u32[]{:S(2)}) collective-permute-start(bf16[512,128]{1,0:T(8,128)(2,1)S(1)} %constant_dynamic-update-slice_fusion.pair_ref), channel_id=1, source_target_pairs={{0,2},{1,5},{2,0},{3,7},{4,6},{5,1},{6,4},{7,3},{8,10},{9,13},{10,... | collective-permute-start | bytes 393224 | tf_op jit(solution)/shard_map/ppermute | solution.py:464
  49.8 0.0 collective-permute-done.13.far_ref
  49.8 3.3 %collective-permute-done.12.near_ref = bf16[512,128]{1,0:T(8,128)(2,1)S(1)} collective-permute-done((bf16[512,128]{1,0:T(8,128)(2,1)S(1)}, bf16[512,128]{1,0:T(8,128)(2,1)S(1)}, u32[]{:S(2)}, u32[]{:S(2)}) %collective-permute-start.12) | collective-permute-done | bytes 131104 | tf_op jit(solution)/shard_map/ppermute | solution.py:464
  53.1 0.3 half_slab.1.refs_0_
  53.4 0.5 collective-permute-start.16
  54.0 1.5 %collective-permute-start.15 = (bf16[16,8192]{1,0:T(8,128)(2,1)S(1)}, bf16[16,8192]{1,0:T(8,128)(2,1)S(1)}, u32[]{:S(2)}, u32[]{:S(2)}) collective-permute-start(bf16[16,8192]{1,0:T(8,128)(2,1)S(1)} %half_slab.1.refs_0_), channel_id=1, source_target_pairs={{0,16},{1,17},{2,18},{3,19},{4,20},{5,21},{6,22},{7,23},{8,24},{9,... | collective-permute-start | bytes 786440 | tf_op jit(solution)/shard_map/ppermute | solution.py:464
  55.5 1.5 %collective-permute-start.14 = (bf16[16,8192]{1,0:T(8,128)(2,1)S(1)}, bf16[16,8192]{1,0:T(8,128)(2,1)S(1)}, u32[]{:S(2)}, u32[]{:S(2)}) collective-permute-start(bf16[16,8192]{1,0:T(8,128)(2,1)S(1)} %half_slab.1.refs_0_), channel_id=1, source_target_pairs={{0,8},{1,9},{2,10},{3,11},{4,12},{5,13},{6,14},{7,15},{8,0},{9,1},... | collective-permute-start | bytes 786440 | tf_op jit(solution)/shard_map/ppermute | solution.py:464
  57.0 4.8 %collective-permute-start.17 = (bf16[16,8192]{1,0:T(8,128)(2,1)S(1)}, bf16[16,8192]{1,0:T(8,128)(2,1)S(1)}, u32[]{:S(2)}, u32[]{:S(2)}) collective-permute-start(bf16[16,8192]{1,0:T(8,128)(2,1)S(1)} %half_slab.1.refs_0_), channel_id=1, source_target_pairs={{0,1},{1,0},{2,3},{3,2},{4,5},{5,4},{6,7},{7,6},{8,9},{9,8},{10,11... | collective-permute-start | bytes 786440 | tf_op jit(solution)/shard_map/ppermute | solution.py:464
  61.8 0.0 collective-permute-done.16.refs_3_
  61.8 4.6 %collective-permute-start.20 = (bf16[16,8192]{1,0:T(8,128)(2,1)S(1)}, bf16[16,8192]{1,0:T(8,128)(2,1)S(1)}, u32[]{:S(2)}, u32[]{:S(2)}) collective-permute-start(bf16[16,8192]{1,0:T(8,128)(2,1)S(1)} %collective-permute-done.16.refs_3_), channel_id=1, source_target_pairs={{0,1},{1,0},{2,3},{3,2},{4,5},{5,4},{6,7},{7,6},{8,9},{9,8},{10,11... | collective-permute-start | bytes 786440 | tf_op jit(solution)/shard_map/ppermute | solution.py:464
  66.4 0.9 %collective-permute-done.15.refs_2_ = bf16[16,8192]{1,0:T(8,128)(2,1)S(1)} collective-permute-done((bf16[16,8192]{1,0:T(8,128)(2,1)S(1)}, bf16[16,8192]{1,0:T(8,128)(2,1)S(1)}, u32[]{:S(2)}, u32[]{:S(2)}) %collective-permute-start.15) | collective-permute-done | bytes 262176 | tf_op jit(solution)/shard_map/ppermute | solution.py:464
  67.2 1.4 %collective-permute-start.19 = (bf16[16,8192]{1,0:T(8,128)(2,1)S(1)}, bf16[16,8192]{1,0:T(8,128)(2,1)S(1)}, u32[]{:S(2)}, u32[]{:S(2)}) collective-permute-start(bf16[16,8192]{1,0:T(8,128)(2,1)S(1)} %collective-permute-done.15.refs_2_), channel_id=1, source_target_pairs={{0,1},{1,0},{2,3},{3,2},{4,5},{5,4},{6,7},{7,6},{8,9},{9,8},{10,11... | collective-permute-start | bytes 786440 | tf_op jit(solution)/shard_map/ppermute | solution.py:464
  68.6 0.0 collective-permute-done.14.refs_1_
  68.6 0.0 collective-permute-start.18
  68.6 0.0 collective-permute-done.17.refs_4_
  68.6 0.0 collective-permute-done.20.refs_7_
  68.6 1.1 %collective-permute-done.19.refs_6_ = bf16[16,8192]{1,0:T(8,128)(2,1)S(1)} collective-permute-done((bf16[16,8192]{1,0:T(8,128)(2,1)S(1)}, bf16[16,8192]{1,0:T(8,128)(2,1)S(1)}, u32[]{:S(2)}, u32[]{:S(2)}) %collective-permute-start.19) | collective-permute-done | bytes 262176 | tf_op jit(solution)/shard_map/ppermute | solution.py:464
  69.8 0.4 collective-permute-done.18.refs_5_
  70.2 1.4 %place_slabs.1 = bf16[128,8192]{1,0:T(8,128)(2,1)} custom-call(bf16[16,8192]{1,0:T(8,128)(2,1)S(1)} %half_slab.1.refs_0_, bf16[16,8192]{1,0:T(8,128)(2,1)S(1)} %collective-permute-done.14.refs_1_, bf16[16,8192]{1,0:T(8,128)(2,1)S(1)} %collective-permute-done.15.refs_2_, bf16[16,8192]{1,0:T(8,128)(2,1)S(1)} %collective-permute-done.16.refs_3_, ...), custom_call_target="tpu_custom_call" | custom-call | tf_op jit(solution)/shard_map/place_slabs/pallas_call | solution.py:444
  (4 shorter events, 0.0 us)
Async XLA Ops:
  0.6 3.7 %copy-start.6 = (s32[2,128]{1,0:T(2,128)S(1)}, s32[2,128]{1,0:T(2,128)}, u32[]{:S(2)}) copy-start(s32[2,128]{1,0:T(2,128)} %signs_ref.1) | copy-start | bytes 3076
  0.6 3.7 %copy-start = (bf16[128,8192]{1,0:T(8,128)(2,1)S(1)}, bf16[128,8192]{1,0:T(8,128)(2,1)}, u32[]{:S(2)}) copy-start(bf16[128,8192]{1,0:T(8,128)(2,1)} %grads_hbm.7) | copy-start | bytes 6291460
  0.7 3.7 %copy-start.2 = (bf16[128,128]{1,0:T(8,128)(2,1)S(1)}, bf16[128,128]{1,0:T(8,128)(2,1)}, u32[]{:S(2)}) copy-start(bf16[128,128]{1,0:T(8,128)(2,1)} %acts_hbm.7) | copy-start | bytes 98308
  0.7 3.7 %copy-start.1 = (s32[8192]{0:T(1024)S(1)}, s32[8192]{0:T(1024)}, u32[]{:S(2)}) copy-start(s32[8192]{0:T(1024)} %param.10) | copy-start | bytes 98308
  3.8 3.0 %collective-permute-start = (bf16[2048,128]{1,0:T(8,128)(2,1)}, bf16[2048,128]{1,0:T(8,128)(2,1)S(1)}, u32[]{:S(2)}, u32[]{:S(2)}) collective-permute-start(bf16[2048,128]{1,0:T(8,128)(2,1)} %front_theirs.2), channel_id=1, source_target_pairs={{0,1},{1,0},{2,3},{3,2},{4,5},{5,4},{6,7},{7,6},{8,9},{9,8},{10,11... | collective-permute-start | bytes 1572872 | tf_op jit(solution)/shard_map/ppermute | solution.py:464
  5.5 8.3 %collective-permute-start.4 = (bf16[2048,128]{1,0:T(8,128)(2,1)S(1)}, bf16[2048,128]{1,0:T(8,128)(2,1)S(1)}, u32[]{:S(2)}, u32[]{:S(2)}) collective-permute-start(bf16[2048,128]{1,0:T(8,128)(2,1)S(1)} %front_theirs.3), channel_id=1, source_target_pairs={{0,1},{1,0},{2,3},{3,2},{4,5},{5,4},{6,7},{7,6},{8,9},{9,8},{10,11... | collective-permute-start | bytes 1572872 | tf_op jit(solution)/shard_map/ppermute | solution.py:464
  6.9 28.1 %copy-start.3 = (s32[8192]{0:T(1024)S(1)}, s32[8192]{0:T(1024)}, u32[]{:S(2)}) copy-start(s32[8192]{0:T(1024)} %param.11) | copy-start | bytes 98308
  6.9 37.1 %copy-start.4 = (f32[256,128]{1,0:T(8,128)S(1)}, f32[256,128]{1,0:T(8,128)}, u32[]{:S(2)}) copy-start(f32[256,128]{1,0:T(8,128)} %momentum_ref.1) | copy-start | bytes 393220
  6.9 37.1 %copy-start.5 = (s32[8192]{0:T(1024)S(1)}, s32[8192]{0:T(1024)}, u32[]{:S(2)}) copy-start(s32[8192]{0:T(1024)} %param.12) | copy-start | bytes 98308
  6.9 11.5 %collective-permute-start.1 = (bf16[512,128]{1,0:T(8,128)(2,1)S(1)}, bf16[512,128]{1,0:T(8,128)(2,1)S(1)}, u32[]{:S(2)}, u32[]{:S(2)}) collective-permute-start(bf16[512,128]{1,0:T(8,128)(2,1)S(1)} %get-tuple-element.17), channel_id=1, source_target_pairs={{0,2},{1,3},{2,0},{3,1},{4,6},{5,7},{6,4},{7,5},{8,10},{9,11},{10,... | collective-permute-start | bytes 393224 | tf_op jit(solution)/shard_map/ppermute | solution.py:464
  11.1 13.0 %collective-permute-start.2 = (bf16[512,128]{1,0:T(8,128)(2,1)S(1)}, bf16[512,128]{1,0:T(8,128)(2,1)S(1)}, u32[]{:S(2)}, u32[]{:S(2)}) collective-permute-start(bf16[512,128]{1,0:T(8,128)(2,1)S(1)} %get-tuple-element.18), channel_id=1, source_target_pairs={{0,4},{1,5},{2,6},{3,7},{4,0},{5,1},{6,2},{7,3},{8,12},{9,13},{10,... | collective-permute-start | bytes 393224 | tf_op jit(solution)/shard_map/ppermute | solution.py:464
  13.8 10.3 %collective-permute-start.3 = (bf16[512,128]{1,0:T(8,128)(2,1)S(1)}, bf16[512,128]{1,0:T(8,128)(2,1)S(1)}, u32[]{:S(2)}, u32[]{:S(2)}) collective-permute-start(bf16[512,128]{1,0:T(8,128)(2,1)S(1)} %get-tuple-element.19), channel_id=1, source_target_pairs={{0,6},{1,7},{2,4},{3,5},{4,2},{5,3},{6,0},{7,1},{8,14},{9,15},{10,... | collective-permute-start | bytes 393224 | tf_op jit(solution)/shard_map/ppermute | solution.py:464
  13.9 10.2 %collective-permute-start.5 = (bf16[512,128]{1,0:T(8,128)(2,1)S(1)}, bf16[512,128]{1,0:T(8,128)(2,1)S(1)}, u32[]{:S(2)}, u32[]{:S(2)}) collective-permute-start(bf16[512,128]{1,0:T(8,128)(2,1)S(1)} %get-tuple-element.21), channel_id=1, source_target_pairs={{0,2},{1,3},{2,0},{3,1},{4,6},{5,7},{6,4},{7,5},{8,10},{9,11},{10,... | collective-permute-start | bytes 393224 | tf_op jit(solution)/shard_map/ppermute | solution.py:464
  14.9 20.1 %collective-permute-start.6 = (bf16[512,128]{1,0:T(8,128)(2,1)S(1)}, bf16[512,128]{1,0:T(8,128)(2,1)S(1)}, u32[]{:S(2)}, u32[]{:S(2)}) collective-permute-start(bf16[512,128]{1,0:T(8,128)(2,1)S(1)} %get-tuple-element.22), channel_id=1, source_target_pairs={{0,4},{1,5},{2,6},{3,7},{4,0},{5,1},{6,2},{7,3},{8,12},{9,13},{10,... | collective-permute-start | bytes 393224 | tf_op jit(solution)/shard_map/ppermute | solution.py:464
  18.4 16.6 %collective-permute-start.7 = (bf16[512,128]{1,0:T(8,128)(2,1)S(1)}, bf16[512,128]{1,0:T(8,128)(2,1)S(1)}, u32[]{:S(2)}, u32[]{:S(2)}) collective-permute-start(bf16[512,128]{1,0:T(8,128)(2,1)S(1)} %get-tuple-element.23), channel_id=1, source_target_pairs={{0,6},{1,7},{2,4},{3,5},{4,2},{5,3},{6,0},{7,1},{8,14},{9,15},{10,... | collective-permute-start | bytes 393224 | tf_op jit(solution)/shard_map/ppermute | solution.py:464
  35.8 4.8 %collective-permute-start.8 = (bf16[256,128]{1,0:T(8,128)(2,1)S(1)}, bf16[256,128]{1,0:T(8,128)(2,1)S(1)}, u32[]{:S(2)}, u32[]{:S(2)}) collective-permute-start(bf16[256,128]{1,0:T(8,128)(2,1)S(1)} %get-tuple-element.25), channel_id=1, source_target_pairs={{0,8},{1,9},{2,10},{3,11},{4,12},{5,13},{6,14},{7,15},{8,0},{9,1},... | collective-permute-start | bytes 196616 | tf_op jit(solution)/shard_map/ppermute | solution.py:464
  37.3 4.5 %collective-permute-start.9 = (bf16[256,128]{1,0:T(8,128)(2,1)S(1)}, bf16[256,128]{1,0:T(8,128)(2,1)S(1)}, u32[]{:S(2)}, u32[]{:S(2)}) collective-permute-start(bf16[256,128]{1,0:T(8,128)(2,1)S(1)} %get-tuple-element.26), channel_id=1, source_target_pairs={{0,16},{1,17},{2,18},{3,19},{4,20},{5,21},{6,22},{7,23},{8,24},{9,... | collective-permute-start | bytes 196616 | tf_op jit(solution)/shard_map/ppermute | solution.py:464
  38.8 5.2 %collective-permute-start.10 = (bf16[256,128]{1,0:T(8,128)(2,1)S(1)}, bf16[256,128]{1,0:T(8,128)(2,1)S(1)}, u32[]{:S(2)}, u32[]{:S(2)}) collective-permute-start(bf16[256,128]{1,0:T(8,128)(2,1)S(1)} %get-tuple-element.27), channel_id=1, source_target_pairs={{0,24},{1,25},{2,26},{3,27},{4,28},{5,29},{6,30},{7,31},{8,16},{9,... | collective-permute-start | bytes 196616 | tf_op jit(solution)/shard_map/ppermute | solution.py:464
  45.2 1.3 %collective-permute-start.11 = (bf16[256,128]{1,0:T(8,128)(2,1)S(1)}, bf16[256,128]{1,0:T(8,128)(2,1)S(1)}, u32[]{:S(2)}, u32[]{:S(2)}) collective-permute-start(bf16[256,128]{1,0:T(8,128)(2,1)S(1)} %get-tuple-element.29), channel_id=1, source_target_pairs={{0,1},{1,0},{2,3},{3,2},{4,5},{5,4},{6,7},{7,6},{8,9},{9,8},{10,11... | collective-permute-start | bytes 196616 | tf_op jit(solution)/shard_map/ppermute | solution.py:464
  46.5 3.2 %collective-permute-start.13 = (bf16[512,128]{1,0:T(8,128)(2,1)S(1)}, bf16[512,128]{1,0:T(8,128)(2,1)S(1)}, u32[]{:S(2)}, u32[]{:S(2)}) collective-permute-start(bf16[512,128]{1,0:T(8,128)(2,1)S(1)} %constant_dynamic-update-slice_fusion.pair_ref), channel_id=1, source_target_pairs={{1,7},{3,5},{5,3},{7,1},{9,15},{11,13},{13,11},{15,9},{17,23},{19,... | collective-permute-start | bytes 393224 | tf_op jit(solution)/shard_map/ppermute | solution.py:464
  47.2 5.9 %collective-permute-start.12 = (bf16[512,128]{1,0:T(8,128)(2,1)S(1)}, bf16[512,128]{1,0:T(8,128)(2,1)S(1)}, u32[]{:S(2)}, u32[]{:S(2)}) collective-permute-start(bf16[512,128]{1,0:T(8,128)(2,1)S(1)} %constant_dynamic-update-slice_fusion.pair_ref), channel_id=1, source_target_pairs={{0,2},{1,5},{2,0},{3,7},{4,6},{5,1},{6,4},{7,3},{8,10},{9,13},{10,... | collective-permute-start | bytes 393224 | tf_op jit(solution)/shard_map/ppermute | solution.py:464
  53.4 8.3 %collective-permute-start.16 = (bf16[16,8192]{1,0:T(8,128)(2,1)S(1)}, bf16[16,8192]{1,0:T(8,128)(2,1)S(1)}, u32[]{:S(2)}, u32[]{:S(2)}) collective-permute-start(bf16[16,8192]{1,0:T(8,128)(2,1)S(1)} %half_slab.1.refs_0_), channel_id=1, source_target_pairs={{0,24},{1,25},{2,26},{3,27},{4,28},{5,29},{6,30},{7,31},{8,16},{9,... | collective-permute-start | bytes 786440 | tf_op jit(solution)/shard_map/ppermute | solution.py:464
  54.0 13.2 %collective-permute-start.15 = (bf16[16,8192]{1,0:T(8,128)(2,1)S(1)}, bf16[16,8192]{1,0:T(8,128)(2,1)S(1)}, u32[]{:S(2)}, u32[]{:S(2)}) collective-permute-start(bf16[16,8192]{1,0:T(8,128)(2,1)S(1)} %half_slab.1.refs_0_), channel_id=1, source_target_pairs={{0,16},{1,17},{2,18},{3,19},{4,20},{5,21},{6,22},{7,23},{8,24},{9,... | collective-permute-start | bytes 786440 | tf_op jit(solution)/shard_map/ppermute | solution.py:464
  55.5 13.1 %collective-permute-start.14 = (bf16[16,8192]{1,0:T(8,128)(2,1)S(1)}, bf16[16,8192]{1,0:T(8,128)(2,1)S(1)}, u32[]{:S(2)}, u32[]{:S(2)}) collective-permute-start(bf16[16,8192]{1,0:T(8,128)(2,1)S(1)} %half_slab.1.refs_0_), channel_id=1, source_target_pairs={{0,8},{1,9},{2,10},{3,11},{4,12},{5,13},{6,14},{7,15},{8,0},{9,1},... | collective-permute-start | bytes 786440 | tf_op jit(solution)/shard_map/ppermute | solution.py:464
  57.0 11.6 %collective-permute-start.17 = (bf16[16,8192]{1,0:T(8,128)(2,1)S(1)}, bf16[16,8192]{1,0:T(8,128)(2,1)S(1)}, u32[]{:S(2)}, u32[]{:S(2)}) collective-permute-start(bf16[16,8192]{1,0:T(8,128)(2,1)S(1)} %half_slab.1.refs_0_), channel_id=1, source_target_pairs={{0,1},{1,0},{2,3},{3,2},{4,5},{5,4},{6,7},{7,6},{8,9},{9,8},{10,11... | collective-permute-start | bytes 786440 | tf_op jit(solution)/shard_map/ppermute | solution.py:464
  61.8 6.9 %collective-permute-start.20 = (bf16[16,8192]{1,0:T(8,128)(2,1)S(1)}, bf16[16,8192]{1,0:T(8,128)(2,1)S(1)}, u32[]{:S(2)}, u32[]{:S(2)}) collective-permute-start(bf16[16,8192]{1,0:T(8,128)(2,1)S(1)} %collective-permute-done.16.refs_3_), channel_id=1, source_target_pairs={{0,1},{1,0},{2,3},{3,2},{4,5},{5,4},{6,7},{7,6},{8,9},{9,8},{10,11... | collective-permute-start | bytes 786440 | tf_op jit(solution)/shard_map/ppermute | solution.py:464
  67.2 2.5 %collective-permute-start.19 = (bf16[16,8192]{1,0:T(8,128)(2,1)S(1)}, bf16[16,8192]{1,0:T(8,128)(2,1)S(1)}, u32[]{:S(2)}, u32[]{:S(2)}) collective-permute-start(bf16[16,8192]{1,0:T(8,128)(2,1)S(1)} %collective-permute-done.15.refs_2_), channel_id=1, source_target_pairs={{0,1},{1,0},{2,3},{3,2},{4,5},{5,4},{6,7},{7,6},{8,9},{9,8},{10,11... | collective-permute-start | bytes 786440 | tf_op jit(solution)/shard_map/ppermute | solution.py:464
  68.6 1.5 %collective-permute-start.18 = (bf16[16,8192]{1,0:T(8,128)(2,1)S(1)}, bf16[16,8192]{1,0:T(8,128)(2,1)S(1)}, u32[]{:S(2)}, u32[]{:S(2)}) collective-permute-start(bf16[16,8192]{1,0:T(8,128)(2,1)S(1)} %collective-permute-done.14.refs_1_), channel_id=1, source_target_pairs={{0,1},{1,0},{2,3},{3,2},{4,5},{5,4},{6,7},{7,6},{8,9},{9,8},{10,11... | collective-permute-start | bytes 786440 | tf_op jit(solution)/shard_map/ppermute | solution.py:464
where the time goes:
time: 71.7 us; the launch traced here: 71.5 us
  starting transfers between devices  32.1 us (45%)
  waiting for transfers between devices  28.1 us (39%)
  Pallas kernels  10.4 us (15%)
  between operations  0.8 us (1%)
    ppermute x21, starting transfers between devices, send(): return lax.ppermute(value, ('outer', 'inner'), pairs)  32.1 us
    ppermute x21, waiting for transfers between devices, send(): return lax.ppermute(value, ('outer', 'inner'), pairs)  28.1 us
    pallas_call x4, Pallas kernels, front(): pl.pallas_call(kernel, out_shape=jax.ShapeDtypeStruct((plan.levels * chun...  6.46 us
  transfers between devices with their start and end apart: 21, of which 10 were waited for; matrix products, arithmetic and copies ran while one was open for 0% of the time, Pallas kernels for 5%

commit v1 on v0

--- a/solution.py
+++ b/solution.py
@@ -117,6 +117,7 @@
             and self.own_rows * self.outer * self.inner == self.rows
             and self.seg_rows == 16
             and self.slab_rows == 16
+            and self.outer == 4
             and self.order == 128
             and 2 * self.chunks == self.order
         )
@@ -261,13 +262,26 @@
     )(ours, theirs)
 
 
+def add_pieces(one, two):
+    def kernel(one_ref, two_ref, out):
+        total = one_ref[...].astype(jnp.float32) + two_ref[...].astype(jnp.float32)
+        out[...] = total.astype(jnp.bfloat16)
+
+    return pl.pallas_call(
+        kernel,
+        out_shape=jax.ShapeDtypeStruct(one.shape, one.dtype),
+        compiler_params=vmem(8),
+        name="add_pieces",
+    )(one, two)
+
+
 def requantize(plan, spans, first_exp, second_exp, parts):
     first_chunk, chunk_count = whole_span(spans)
     seg = plan.seg_rows
-    levels = plan.levels
+    pieces = len(parts[0])
 
     def kernel(first_ref, second_ref, *refs):
-        ins, outs = refs[: levels * len(spans)], refs[levels * len(spans) :]
+        ins, outs = refs[: pieces * len(spans)], refs[pieces * len(spans) :]
         outer_place, level, core = places()
         index = iota((seg, 1), 0)
         own = index & (plan.own_rows - 1)
@@ -283,8 +297,8 @@
             order = jnp.where(there == source, 1.0, 0.0).astype(jnp.bfloat16)
             for step in range(span_count // group):
                 rows = pl.ds(step * size, size)
-                total = ins[n * levels][rows, :].astype(jnp.float32)
-                for other in ins[n * levels + 1 : (n + 1) * levels]:
+                total = ins[n * pieces][rows, :].astype(jnp.float32)
+                for other in ins[n * pieces + 1 : (n + 1) * pieces]:
                     total = total + other[rows, :].astype(jnp.float32)
                 start = span_chunk + step * group
                 scaled = jnp.concatenate(
@@ -374,82 +388,96 @@
     )(second_exp, third_exp, signs, momentum, *parts)
 
 
-def band_of(level, core):
-    return core ^ (level >> 1)
-
-
-def half_slab(plan, span, pair, near, far):
+def chip_slab(plan, span, ours, theirs):
     _, chunk_count = span
-    own_rows, rows = plan.own_rows, plan.slab_rows
+    own_rows = plan.own_rows
+    rows = 2 * own_rows
     group = tile(chunk_count, 16)
     size = group * rows
 
-    def kernel(pair_ref, near_ref, far_ref, out):
-        _, level, core = places()
+    def kernel(ours_ref, theirs_ref, out):
+        _, _, core = places()
         here, there = iota((size, size), 0), iota((size, size), 1)
         row = here & (rows - 1)
-        device = row >> log2(own_rows)
-        side = ((device >> 1) ^ level) & 1
-        part = 2 * side + ((device ^ core) & 1)
+        part = (row >> log2(own_rows)) ^ core
         source = (part * own_rows + (row & (own_rows - 1))) * group + (here >> log2(rows))
         order = jnp.where(there == source, 1.0, 0.0).astype(jnp.bfloat16)
-        lower = core == 0
         for step in range(chunk_count // group):
-            blocks = []
-            for one, two in ((pair_ref, near_ref), (near_ref, far_ref)):
-                for k in range(2 * own_rows):
-                    at = pl.ds(k * chunk_count + step * group, group)
-                    blocks.append(jnp.where(lower, one[at, :], two[at, :]))
-            block = jnp.concatenate(blocks, axis=0)
+            block = jnp.concatenate(
+                [
+                    part_ref[pl.ds(k * chunk_count + step * group, group), :]
+                    for part_ref in (ours_ref, theirs_ref)
+                    for k in range(own_rows)
+                ],
+                axis=0,
+            )
             moved = jnp.dot(order, block, preferred_element_type=jnp.float32).astype(jnp.bfloat16)
             for c in range(group):
                 at = (step * group + c) * plan.order
                 out[:, pl.ds(at, plan.order)] = moved[c * rows : (c + 1) * rows]
 
-    shape = jax.ShapeDtypeStruct((rows, chunk_count * plan.order), jnp.bfloat16)
-    return pl.pallas_call(
-        kernel, out_shape=shape, compiler_params=vmem(8), name="half_slab"
-    )(pair, near, far)
-
-
-def place_slabs(plan, ours, theirs):
-    spans = plan.spans
-
+    return pl.pallas_call(
+        kernel,
+        out_shape=jax.ShapeDtypeStruct((rows, plan.width), jnp.bfloat16),
+        compiler_params=vmem(8),
+        name="chip_slab",
+    )(ours, theirs)
+
+
+def band_of(level, core):
+    return core ^ (level >> 1)
+
+
+def band_slab(plan, own, near, far):
+    def kernel(own_ref, near_ref, far_ref, out):
+        _, level, core = places()
+        lower, odd = core == 0, (level & 1) == 1
+        step = 8 * plan.order
+        for at in range(0, plan.width, step):
+            cut = pl.ds(at, step)
+            near_part = near_ref[:, cut]
+            same = jnp.where(lower, own_ref[:, cut], near_part)
+            other = jnp.where(lower, near_part, far_ref[:, cut])
+            rows = jnp.concatenate(
+                [jnp.where(odd, other, same), jnp.where(odd, same, other)], axis=0
+            )
+            out[:, cut] = rows
+
+    return pl.pallas_call(
+        kernel,
+        out_shape=jax.ShapeDtypeStruct((plan.slab_rows, plan.width), jnp.bfloat16),
+        compiler_params=vmem(8),
+        name="band_slab",
+    )(own, near, far)
+
+
+def place_slabs(plan, whole, pieces):
     def kernel(*refs):
-        (out, sems), ins = refs[-2:], refs[:-2]
+        (out, sems), ins = refs[-2:], refs[: len(pieces)]
         outer_place, level, core = places()
         copies = []
-        for n, (first_chunk, chunk_count) in enumerate(spans):
-            for side in range(2):
-                band = band_of(level, core) if side == 0 else 1 - band_of(level, core)
-                for hop in range(plan.outer):
-                    at = (n * 2 + side) * plan.outer + hop
-                    row = ((outer_place ^ hop) * 2 + band) * plan.slab_rows
-                    copies.append(
-                        pltpu.make_async_copy(
-                            ins[at],
-                            out.at[
-                                pl.ds(row, plan.slab_rows),
-                                pl.ds(first_chunk * plan.order, chunk_count * plan.order),
-                            ],
-                            sems.at[at],
-                        )
-                    )
+        for n, (hop, mine, piece) in enumerate(pieces):
+            band = band_of(level, core) if mine else 1 - band_of(level, core)
+            row = ((outer_place ^ hop) * 2 + band) * plan.slab_rows
+            copies.append(
+                pltpu.make_async_copy(ins[n], out.at[pl.ds(row, plan.slab_rows), :], sems.at[n])
+            )
         for copy in copies:
             copy.start()
         for copy in copies:
             copy.wait()
 
-    flat = [piece for n in range(len(spans)) for side in (ours[n], theirs[n]) for piece in side]
+    before = [] if whole is None else [whole]
     return pl.pallas_call(
         kernel,
         out_shape=jax.ShapeDtypeStruct((plan.rows, plan.width), jnp.bfloat16),
-        in_specs=[pl.BlockSpec(memory_space=pl.ANY)] * len(flat),
+        in_specs=[pl.BlockSpec(memory_space=pl.ANY)] * (len(pieces) + len(before)),
         out_specs=pl.BlockSpec(memory_space=pl.ANY),
-        scratch_shapes=[pltpu.SemaphoreType.DMA((len(flat),))],
+        scratch_shapes=[pltpu.SemaphoreType.DMA((len(pieces),))],
+        input_output_aliases={len(pieces): 0} if before else {},
         compiler_params=vmem(8),
         name="place_slabs",
-    )(*flat)
+    )(*[piece for hop, mine, piece in pieces], *before)
 
 
 def send(plan, value, target_of):
@@ -489,13 +517,14 @@
     theirs = swap_cores(plan, theirs)
     ours = front(plan, span, True, activations, out_grads, first_exp, signs)
     joined = join_cores(plan, ours, theirs)
-    parts = [joined[0]]
-    for hop in range(1, plan.levels):
-        parts.append(over_levels(plan, joined[hop], hop))
-    return parts
-
-
-def stream_back(plan, spans, tables, momentum, parts):
+    passed = over_levels(plan, joined[3], 1)
+    passed = add_pieces(passed, joined[2])
+    far = over_levels(plan, passed, 2)
+    near = over_levels(plan, joined[1], 1)
+    return [joined[0], near, far]
+
+
+def stream_owner(plan, spans, tables, momentum, parts):
     first_exp, second_exp, third_exp, signs = tables
     span = whole_span(spans)
     parts = requantize(plan, spans, first_exp, second_exp, parts)
@@ -503,17 +532,28 @@
     for hop in range(1, plan.outer):
         pieces.append(over_outer(plan, parts[hop], hop))
     moment, update = owner(plan, span, second_exp, third_exp, signs, momentum, pieces)
-    pair = jnp.concatenate([update, swap_cores(plan, update)], axis=0)
-    near = to_near(plan, pair)
-    far = to_far(plan, pair)
-    slab = half_slab(plan, span, pair, near, far)
-    ours = [slab]
+    return moment, update, swap_cores(plan, update)
+
+
+def gather(plan, span, ours, theirs):
+    chip = chip_slab(plan, span, ours, theirs)
+    near = to_near(plan, chip)
+    far = to_far(plan, chip)
+    slab = band_slab(plan, chip, near, far)
+    mine, other = [slab], []
     for hop in range(1, plan.outer):
-        ours.append(over_outer(plan, slab, hop))
-    theirs = []
+        mine.append(over_outer(plan, slab, hop))
     for hop in range(plan.outer):
-        theirs.append(swap_cores(plan, ours[hop]))
-    return moment, ours, theirs
+        other.append(swap_cores(plan, mine[hop]))
+    whole = None
+    for ready in STAGES:
+        whole = place_slabs(
+            plan, whole, [p for h in ready for p in ((h, True, mine[h]), (h, False, other[h]))]
+        )
+    return whole
+
+
+STAGES = ((0, 3), (2, 1))
 
 
 def on_device(activations, out_grads, momentum, first_exp, second_exp, third_exp, signs):
@@ -521,25 +561,16 @@
     if not plan.fits():
         return general(activations, out_grads, momentum, first_exp, second_exp, third_exp, signs)
     exps = [e.reshape(-1, plan.order) for e in (first_exp, second_exp, third_exp)]
-    groups = split_chunks(plan.chunks)
-    plan.spans = [whole_span(spans) for spans in groups]
-    fronts = {}
-    for spans in groups:
-        for span in spans:
-            fronts[span] = stream_front(plan, span, activations, out_grads, exps[0], signs)
-    done = [
-        stream_back(plan, spans, (*exps, signs), momentum, [fronts[span] for span in spans])
-        for spans in groups
-    ]
-    moments = [d[0].reshape(plan.own_rows, -1, plan.order) for d in done]
-    new_momentum = jnp.concatenate(moments, axis=1).reshape(momentum.shape)
-    update = place_slabs(plan, [d[1] for d in done], [d[2] for d in done])
+    spans = split_chunks(plan.chunks)
+    fronts = [stream_front(plan, span, activations, out_grads, exps[0], signs) for span in spans]
+    new_momentum, ours, theirs = stream_owner(plan, spans, (*exps, signs), momentum, fronts)
+    update = gather(plan, whole_span(spans), ours, theirs)
     return (new_momentum, update)
 
 
 def split_chunks(chunks):
-    half = chunks // 2
-    return [[(0, half), (half, chunks - half)]]
+    first = 5 * chunks // 8
+    return [(0, first), (first, chunks - first)]
 
 
 def solution(mesh):

time: 71.7 us -> 64.5 us (0.90)
  waiting for transfers between devices: 28.1 us -> 18.5 us
  starting transfers between devices: 32.1 us -> 33.4 us
  Pallas kernels: 10.4 us -> 11.6 us
    ppermute x21, waiting for transfers between devices: 28.1 us -> 18.5 us  [send(): return lax.ppermute(value, ('outer', 'inner'), pairs)]
    ppermute x21, starting transfers between devices: 32.1 us -> 33.4 us  [send(): return lax.ppermute(value, ('outer', 'inner'), pairs)]
    pallas_call x1 -> x2, Pallas kernels: 1.37 us -> 1.99 us  [place_slabs(): pl.pallas_call(kernel, out_shape=jax.ShapeDtypeStruct((plan.rows, plan.wi...]
  transfers between devices with their start and end apart: 21 -> 21, of which waited for: 10 -> 8; matrix products, arithmetic and copies ran while one was open for 0% -> 0% of each run, Pallas kernels for 5% -> 8%
where the time goes in v1:
time: 64.5 us; the launch traced here: 64.4 us
  starting transfers between devices  33.4 us (52%)
  waiting for transfers between devices  18.5 us (29%)
  Pallas kernels  11.6 us (18%)
  between operations  0.83 us (1%)
    ppermute x21, starting transfers between devices, send(): return lax.ppermute(value, ('outer', 'inner'), pairs)  33.4 us
    ppermute x21, waiting for transfers between devices, send(): return lax.ppermute(value, ('outer', 'inner'), pairs)  18.5 us
    pallas_call x4, Pallas kernels, front(): pl.pallas_call(kernel, out_shape=jax.ShapeDtypeStruct((plan.levels * chun...  7.16 us
    pallas_call x2, Pallas kernels, place_slabs(): pl.pallas_call(kernel, out_shape=jax.ShapeDtypeStruct((plan.rows, plan.wi...  1.99 us
  transfers between devices with their start and end apart: 21, of which 8 were waited for; matrix products, arithmetic and copies ran while one was open for 0% of the time, Pallas kernels for 8%

profile of v1, /device:TPU:0, one launch (start us, length us, event | category | flops | bytes accessed | tf_op | source)
XLA Modules:
  0.0 64.4 jit_solution(799354865378689621)
XLA Ops:
  0.6 0.0 copy-start.6
  0.6 0.0 copy-start
  0.7 0.0 copy-start.2
  0.7 0.0 copy-start.1
  0.7 3.5 %front_theirs.2 = bf16[2560,128]{1,0:T(8,128)(2,1)} custom-call(bf16[128,128]{1,0:T(8,128)(2,1)} %acts_hbm.7, bf16[128,8192]{1,0:T(8,128)(2,1)} %grads_hbm.7, s32[64,128]{1,0:T(8,128)} %bitcast.3, s32[2,128]{1,0:T(2,128)} %signs_ref.1), custom_call_target="tpu_custom_call" | custom-call | tf_op jit(solution)/shard_map/front_theirs/pallas_call | solution.py:231
  4.2 0.6 collective-permute-start
  4.7 0.0 copy-done.6
  4.8 0.0 copy-done.1
  4.8 1.1 %front_theirs.3 = bf16[1536,128]{1,0:T(8,128)(2,1)S(1)} custom-call(bf16[128,128]{1,0:T(8,128)(2,1)S(1)} %copy-done.2, bf16[128,8192]{1,0:T(8,128)(2,1)S(1)} %copy-done, s32[64,128]{1,0:T(8,128)S(1)} %bitcast.4, s32[2,128]{1,0:T(2,128)S(1)} %copy-done.6), custom_call_target="tpu_custom_call" | custom-call | tf_op jit(solution)/shard_map/front_theirs/pallas_call | solution.py:231
  5.9 0.1 collective-permute-start.4
  6.0 1.4 %front_mine.2.one = bf16[2560,128]{1,0:T(8,128)(2,1)S(1)} custom-call(bf16[128,128]{1,0:T(8,128)(2,1)S(1)} %copy-done.2, bf16[128,8192]{1,0:T(8,128)(2,1)S(1)} %copy-done, s32[64,128]{1,0:T(8,128)S(1)} %bitcast.5, s32[2,128]{1,0:T(2,128)S(1)} %copy-done.6), custom_call_target="tpu_custom_call" | custom-call | tf_op jit(solution)/shard_map/front_mine/pallas_call | solution.py:231
  7.4 0.0 collective-permute-done.two
  7.4 0.2 join_cores.2
  7.6 0.0 copy-start.4
  7.6 0.0 copy-start.3
  7.6 0.0 copy-start.5
  7.6 3.1 %collective-permute-start.2 = (bf16[640,128]{1,0:T(8,128)(2,1)S(1)}, bf16[640,128]{1,0:T(8,128)(2,1)S(1)}, u32[]{:S(2)}, u32[]{:S(2)}) collective-permute-start(bf16[640,128]{1,0:T(8,128)(2,1)S(1)} %get-tuple-element.18), channel_id=1, source_target_pairs={{0,2},{1,3},{2,0},{3,1},{4,6},{5,7},{6,4},{7,5},{8,10},{9,11},{10,... | collective-permute-start | bytes 491528 | tf_op jit(solution)/shard_map/ppermute | solution.py:492
  10.7 1.1 %front_mine.3.one = bf16[1536,128]{1,0:T(8,128)(2,1)S(1)} custom-call(bf16[128,128]{1,0:T(8,128)(2,1)S(1)} %copy-done.2, bf16[128,8192]{1,0:T(8,128)(2,1)S(1)} %copy-done, s32[64,128]{1,0:T(8,128)S(1)} %bitcast.6, s32[2,128]{1,0:T(2,128)S(1)} %copy-done.6), custom_call_target="tpu_custom_call" | custom-call | tf_op jit(solution)/shard_map/front_mine/pallas_call | solution.py:231
  11.8 0.0 collective-permute-done.4.two
  11.9 0.1 join_cores.3
  12.0 0.1 collective-permute-start.6
  12.1 2.0 %collective-permute-start.1 = (bf16[640,128]{1,0:T(8,128)(2,1)S(1)}, bf16[640,128]{1,0:T(8,128)(2,1)S(1)}, u32[]{:S(2)}, u32[]{:S(2)}) collective-permute-start(bf16[640,128]{1,0:T(8,128)(2,1)S(1)} %get-tuple-element.17), channel_id=1, source_target_pairs={{0,2},{1,3},{2,0},{3,1},{4,6},{5,7},{6,4},{7,5},{8,10},{9,11},{10,... | collective-permute-start | bytes 491528 | tf_op jit(solution)/shard_map/ppermute | solution.py:492
  14.0 1.7 %collective-permute-done.2.one_ref = bf16[640,128]{1,0:T(8,128)(2,1)S(1)} collective-permute-done((bf16[640,128]{1,0:T(8,128)(2,1)S(1)}, bf16[640,128]{1,0:T(8,128)(2,1)S(1)}, u32[]{:S(2)}, u32[]{:S(2)}) %collective-permute-start.2) | collective-permute-done | bytes 163872 | tf_op jit(solution)/shard_map/ppermute | solution.py:492
  15.8 3.1 %collective-permute-start.3 = (bf16[640,128]{1,0:T(8,128)(2,1)S(1)}, bf16[640,128]{1,0:T(8,128)(2,1)S(1)}, u32[]{:S(2)}, u32[]{:S(2)}) collective-permute-start(bf16[640,128]{1,0:T(8,128)(2,1)S(1)} %add_pieces.2), channel_id=1, source_target_pairs={{0,4},{1,5},{2,6},{3,7},{4,0},{5,1},{6,2},{7,3},{8,12},{9,13},{10,... | collective-permute-start | bytes 491528 | tf_op jit(solution)/shard_map/ppermute | solution.py:492
  18.9 1.6 %collective-permute-start.5 = (bf16[384,128]{1,0:T(8,128)(2,1)S(1)}, bf16[384,128]{1,0:T(8,128)(2,1)S(1)}, u32[]{:S(2)}, u32[]{:S(2)}) collective-permute-start(bf16[384,128]{1,0:T(8,128)(2,1)S(1)} %get-tuple-element.21), channel_id=1, source_target_pairs={{0,2},{1,3},{2,0},{3,1},{4,6},{5,7},{6,4},{7,5},{8,10},{9,11},{10,... | collective-permute-start | bytes 294920 | tf_op jit(solution)/shard_map/ppermute | solution.py:492
  20.5 0.0 collective-permute-done.6.one_ref
  20.5 0.5 collective-permute-start.7
  21.0 7.5 %collective-permute-done.5.refs_4_ = bf16[384,128]{1,0:T(8,128)(2,1)S(1)} collective-permute-done((bf16[384,128]{1,0:T(8,128)(2,1)S(1)}, bf16[384,128]{1,0:T(8,128)(2,1)S(1)}, u32[]{:S(2)}, u32[]{:S(2)}) %collective-permute-start.5) | collective-permute-done | bytes 98336 | tf_op jit(solution)/shard_map/ppermute | solution.py:492
  28.5 0.0 collective-permute-done.7.refs_5_
  28.5 0.0 collective-permute-done.1.refs_1_
  28.5 0.0 collective-permute-done.3.refs_2_
  28.5 0.0 copy-done.4
  28.5 0.7 %requantize.1 = (bf16[256,128]{1,0:T(8,128)(2,1)S(1)}, bf16[256,128]{1,0:T(8,128)(2,1)S(1)}, bf16[256,128]{1,0:T(8,128)(2,1)S(1)}, bf16[256,128]{1,0:T(8,128)(2,1)S(1)}) custom-call(s32[64,128]{1,0:T(8,128)S(1)} %bitcast.7, s32[64,128]{1,0:T(8,128)S(1)} %bitcast.8, bf16[640,128]{1,0:T(8,128)(2,1)S(1)} %get-tuple-element.16.refs_0_, ...), custom_call_target="tpu_custom_call" | custom-call | tf_op jit(solution)/shard_map/requantize/pallas_call | solution.py:320
  29.2 1.8 %collective-permute-start.8 = (bf16[256,128]{1,0:T(8,128)(2,1)S(1)}, bf16[256,128]{1,0:T(8,128)(2,1)S(1)}, u32[]{:S(2)}, u32[]{:S(2)}) collective-permute-start(bf16[256,128]{1,0:T(8,128)(2,1)S(1)} %get-tuple-element.25), channel_id=1, source_target_pairs={{0,8},{1,9},{2,10},{3,11},{4,12},{5,13},{6,14},{7,15},{8,0},{9,1},... | collective-permute-start | bytes 196616 | tf_op jit(solution)/shard_map/ppermute | solution.py:492
  31.0 1.5 %collective-permute-start.9 = (bf16[256,128]{1,0:T(8,128)(2,1)S(1)}, bf16[256,128]{1,0:T(8,128)(2,1)S(1)}, u32[]{:S(2)}, u32[]{:S(2)}) collective-permute-start(bf16[256,128]{1,0:T(8,128)(2,1)S(1)} %get-tuple-element.26), channel_id=1, source_target_pairs={{0,16},{1,17},{2,18},{3,19},{4,20},{5,21},{6,22},{7,23},{8,24},{9,... | collective-permute-start | bytes 196616 | tf_op jit(solution)/shard_map/ppermute | solution.py:492
  32.5 0.2 collective-permute-start.10
  32.7 1.0 %collective-permute-done.8.refs_1_ = bf16[256,128]{1,0:T(8,128)(2,1)S(1)} collective-permute-done((bf16[256,128]{1,0:T(8,128)(2,1)S(1)}, bf16[256,128]{1,0:T(8,128)(2,1)S(1)}, u32[]{:S(2)}, u32[]{:S(2)}) %collective-permute-start.8) | collective-permute-done | bytes 65568 | tf_op jit(solution)/shard_map/ppermute | solution.py:492
  33.7 2.0 %collective-permute-done.9.refs_2_ = bf16[256,128]{1,0:T(8,128)(2,1)S(1)} collective-permute-done((bf16[256,128]{1,0:T(8,128)(2,1)S(1)}, bf16[256,128]{1,0:T(8,128)(2,1)S(1)}, u32[]{:S(2)}, u32[]{:S(2)}) %collective-permute-start.9) | collective-permute-done | bytes 65568 | tf_op jit(solution)/shard_map/ppermute | solution.py:492
  35.8 1.9 %collective-permute-done.10.refs_3_ = bf16[256,128]{1,0:T(8,128)(2,1)S(1)} collective-permute-done((bf16[256,128]{1,0:T(8,128)(2,1)S(1)}, bf16[256,128]{1,0:T(8,128)(2,1)S(1)}, u32[]{:S(2)}, u32[]{:S(2)}) %collective-permute-start.10) | collective-permute-done | bytes 65568 | tf_op jit(solution)/shard_map/ppermute | solution.py:492
  37.7 1.2 %owner.1 = (f32[256,128]{1,0:T(8,128)}, bf16[256,128]{1,0:T(8,128)(2,1)S(1)}) custom-call(s32[64,128]{1,0:T(8,128)S(1)} %bitcast.9, s32[64,128]{1,0:T(8,128)S(1)} %bitcast.10, s32[2,128]{1,0:T(2,128)S(1)} %copy-done.6, f32[256,128]{1,0:T(8,128)S(1)} %copy-done.3, bf16[256,128]{1,0:T(8,128)(2,1)S(1)} %get-tuple-element.24.refs_0_, ...), custom_call_target="tpu_custom_call" | custom-call | tf_op jit(solution)/shard_map/owner/pallas_call | solution.py:380
  38.9 0.0 collective-permute-start.11
  38.9 1.3 %collective-permute-done.11.theirs_ref = bf16[256,128]{1,0:T(8,128)(2,1)S(1)} collective-permute-done((bf16[256,128]{1,0:T(8,128)(2,1)S(1)}, bf16[256,128]{1,0:T(8,128)(2,1)S(1)}, u32[]{:S(2)}, u32[]{:S(2)}) %collective-permute-start.11) | collective-permute-done | bytes 65568 | tf_op jit(solution)/shard_map/ppermute | solution.py:492
  40.2 0.2 chip_slab.1.own_ref
  40.3 0.7 %collective-permute-start.13 = (bf16[8,8192]{1,0:T(8,128)(2,1)S(1)}, bf16[8,8192]{1,0:T(8,128)(2,1)S(1)}, u32[]{:S(2)}, u32[]{:S(2)}) collective-permute-start(bf16[8,8192]{1,0:T(8,128)(2,1)S(1)} %chip_slab.1.own_ref), channel_id=1, source_target_pairs={{1,7},{3,5},{5,3},{7,1},{9,15},{11,13},{13,11},{15,9},{17,23},{19,... | collective-permute-start | bytes 393224 | tf_op jit(solution)/shard_map/ppermute | solution.py:492
  41.0 2.6 %collective-permute-start.12 = (bf16[8,8192]{1,0:T(8,128)(2,1)S(1)}, bf16[8,8192]{1,0:T(8,128)(2,1)S(1)}, u32[]{:S(2)}, u32[]{:S(2)}) collective-permute-start(bf16[8,8192]{1,0:T(8,128)(2,1)S(1)} %chip_slab.1.own_ref), channel_id=1, source_target_pairs={{0,2},{1,5},{2,0},{3,7},{4,6},{5,1},{6,4},{7,3},{8,10},{9,13},{10,... | collective-permute-start | bytes 393224 | tf_op jit(solution)/shard_map/ppermute | solution.py:492
  43.6 0.0 collective-permute-done.13.far_ref
  43.6 2.9 %collective-permute-done.12.near_ref = bf16[8,8192]{1,0:T(8,128)(2,1)S(1)} collective-permute-done((bf16[8,8192]{1,0:T(8,128)(2,1)S(1)}, bf16[8,8192]{1,0:T(8,128)(2,1)S(1)}, u32[]{:S(2)}, u32[]{:S(2)}) %collective-permute-start.12) | collective-permute-done | bytes 131104 | tf_op jit(solution)/shard_map/ppermute | solution.py:492
  46.6 0.1 band_slab.1.refs_0_
  46.6 0.5 collective-permute-start.19
  47.2 1.5 %collective-permute-start.16 = (bf16[16,8192]{1,0:T(8,128)(2,1)S(1)}, bf16[16,8192]{1,0:T(8,128)(2,1)S(1)}, u32[]{:S(2)}, u32[]{:S(2)}) collective-permute-start(bf16[16,8192]{1,0:T(8,128)(2,1)S(1)} %band_slab.1.refs_0_), channel_id=1, source_target_pairs={{0,8},{1,9},{2,10},{3,11},{4,12},{5,13},{6,14},{7,15},{8,0},{9,1},... | collective-permute-start | bytes 786440 | tf_op jit(solution)/shard_map/ppermute | solution.py:492
  48.7 1.5 %collective-permute-start.14 = (bf16[16,8192]{1,0:T(8,128)(2,1)S(1)}, bf16[16,8192]{1,0:T(8,128)(2,1)S(1)}, u32[]{:S(2)}, u32[]{:S(2)}) collective-permute-start(bf16[16,8192]{1,0:T(8,128)(2,1)S(1)} %band_slab.1.refs_0_), channel_id=1, source_target_pairs={{0,16},{1,17},{2,18},{3,19},{4,20},{5,21},{6,22},{7,23},{8,24},{9,... | collective-permute-start | bytes 786440 | tf_op jit(solution)/shard_map/ppermute | solution.py:492
  50.2 5.3 %collective-permute-start.18 = (bf16[16,8192]{1,0:T(8,128)(2,1)S(1)}, bf16[16,8192]{1,0:T(8,128)(2,1)S(1)}, u32[]{:S(2)}, u32[]{:S(2)}) collective-permute-start(bf16[16,8192]{1,0:T(8,128)(2,1)S(1)} %band_slab.1.refs_0_), channel_id=1, source_target_pairs={{0,1},{1,0},{2,3},{3,2},{4,5},{5,4},{6,7},{7,6},{8,9},{9,8},{10,11... | collective-permute-start | bytes 786440 | tf_op jit(solution)/shard_map/ppermute | solution.py:492
  55.5 0.0 collective-permute-done.19.refs_2_
  55.5 4.1 %collective-permute-start.20 = (bf16[16,8192]{1,0:T(8,128)(2,1)S(1)}, bf16[16,8192]{1,0:T(8,128)(2,1)S(1)}, u32[]{:S(2)}, u32[]{:S(2)}) collective-permute-start(bf16[16,8192]{1,0:T(8,128)(2,1)S(1)} %collective-permute-done.19.refs_2_), channel_id=1, source_target_pairs={{0,1},{1,0},{2,3},{3,2},{4,5},{5,4},{6,7},{7,6},{8,9},{9,8},{10,11... | collective-permute-start | bytes 786440 | tf_op jit(solution)/shard_map/ppermute | solution.py:492
  59.5 0.0 collective-permute-done.16.refs_2_
  59.5 1.7 %collective-permute-start.17 = (bf16[16,8192]{1,0:T(8,128)(2,1)S(1)}, bf16[16,8192]{1,0:T(8,128)(2,1)S(1)}, u32[]{:S(2)}, u32[]{:S(2)}) collective-permute-start(bf16[16,8192]{1,0:T(8,128)(2,1)S(1)} %collective-permute-done.16.refs_2_), channel_id=1, source_target_pairs={{0,1},{1,0},{2,3},{3,2},{4,5},{5,4},{6,7},{7,6},{8,9},{9,8},{10,11... | collective-permute-start | bytes 786440 | tf_op jit(solution)/shard_map/ppermute | solution.py:492
  61.3 0.0 collective-permute-done.14.refs_0_
  61.3 0.9 %collective-permute-start.15 = (bf16[16,8192]{1,0:T(8,128)(2,1)S(1)}, bf16[16,8192]{1,0:T(8,128)(2,1)S(1)}, u32[]{:S(2)}, u32[]{:S(2)}) collective-permute-start(bf16[16,8192]{1,0:T(8,128)(2,1)S(1)} %collective-permute-done.14.refs_0_), channel_id=1, source_target_pairs={{0,1},{1,0},{2,3},{3,2},{4,5},{5,4},{6,7},{7,6},{8,9},{9,8},{10,11... | collective-permute-start | bytes 786440 | tf_op jit(solution)/shard_map/ppermute | solution.py:492
  62.2 0.0 collective-permute-done.18.refs_1_
  62.2 0.0 collective-permute-done.20.refs_3_
  62.2 1.0 %place_slabs.2.refs_4_ = bf16[128,8192]{1,0:T(8,128)(2,1)} custom-call(bf16[16,8192]{1,0:T(8,128)(2,1)S(1)} %band_slab.1.refs_0_, bf16[16,8192]{1,0:T(8,128)(2,1)S(1)} %collective-permute-done.18.refs_1_, bf16[16,8192]{1,0:T(8,128)(2,1)S(1)} %collective-permute-done.19.refs_2_, bf16[16,8192]{1,0:T(8,128)(2,1)S(1)} %collective-permute-done.20.refs_3_), custom_call_target="tpu_custom_call" | custom-call | tf_op jit(solution)/shard_map/place_slabs/pallas_call | solution.py:471
  63.2 0.0 collective-permute-done.17.refs_3_
  63.2 0.1 collective-permute-done.15.refs_1_
  63.4 1.0 %place_slabs.3 = bf16[128,8192]{1,0:T(8,128)(2,1)} custom-call(bf16[16,8192]{1,0:T(8,128)(2,1)S(1)} %collective-permute-done.14.refs_0_, bf16[16,8192]{1,0:T(8,128)(2,1)S(1)} %collective-permute-done.15.refs_1_, bf16[16,8192]{1,0:T(8,128)(2,1)S(1)} %collective-permute-done.16.refs_2_, ...), custom_call_target="tpu_custom_call", output_to_operand_aliasing={{}: (4, {})} | custom-call | tf_op jit(solution)/shard_map/place_slabs/pallas_call | solution.py:471
  (6 shorter events, 0.1 us)
Async XLA Ops:
  0.6 4.1 %copy-start.6 = (s32[2,128]{1,0:T(2,128)S(1)}, s32[2,128]{1,0:T(2,128)}, u32[]{:S(2)}) copy-start(s32[2,128]{1,0:T(2,128)} %signs_ref.1) | copy-start | bytes 3076
  0.6 4.1 %copy-start = (bf16[128,8192]{1,0:T(8,128)(2,1)S(1)}, bf16[128,8192]{1,0:T(8,128)(2,1)}, u32[]{:S(2)}) copy-start(bf16[128,8192]{1,0:T(8,128)(2,1)} %grads_hbm.7) | copy-start | bytes 6291460
  0.7 4.1 %copy-start.2 = (bf16[128,128]{1,0:T(8,128)(2,1)S(1)}, bf16[128,128]{1,0:T(8,128)(2,1)}, u32[]{:S(2)}) copy-start(bf16[128,128]{1,0:T(8,128)(2,1)} %acts_hbm.7) | copy-start | bytes 98308
  0.7 4.1 %copy-start.1 = (s32[8192]{0:T(1024)S(1)}, s32[8192]{0:T(1024)}, u32[]{:S(2)}) copy-start(s32[8192]{0:T(1024)} %param.10) | copy-start | bytes 98308
  4.2 3.2 %collective-permute-start = (bf16[2560,128]{1,0:T(8,128)(2,1)}, bf16[2560,128]{1,0:T(8,128)(2,1)S(1)}, u32[]{:S(2)}, u32[]{:S(2)}) collective-permute-start(bf16[2560,128]{1,0:T(8,128)(2,1)} %front_theirs.2), channel_id=1, source_target_pairs={{0,1},{1,0},{2,3},{3,2},{4,5},{5,4},{6,7},{7,6},{8,9},{9,8},{10,11... | collective-permute-start | bytes 1966088 | tf_op jit(solution)/shard_map/ppermute | solution.py:492
  5.9 5.9 %collective-permute-start.4 = (bf16[1536,128]{1,0:T(8,128)(2,1)S(1)}, bf16[1536,128]{1,0:T(8,128)(2,1)S(1)}, u32[]{:S(2)}, u32[]{:S(2)}) collective-permute-start(bf16[1536,128]{1,0:T(8,128)(2,1)S(1)} %front_theirs.3), channel_id=1, source_target_pairs={{0,1},{1,0},{2,3},{3,2},{4,5},{5,4},{6,7},{7,6},{8,9},{9,8},{10,11... | collective-permute-start | bytes 1179656 | tf_op jit(solution)/shard_map/ppermute | solution.py:492
  7.6 20.9 %copy-start.4 = (s32[8192]{0:T(1024)S(1)}, s32[8192]{0:T(1024)}, u32[]{:S(2)}) copy-start(s32[8192]{0:T(1024)} %param.11) | copy-start | bytes 98308
  7.6 30.0 %copy-start.3 = (f32[256,128]{1,0:T(8,128)S(1)}, f32[256,128]{1,0:T(8,128)}, u32[]{:S(2)}) copy-start(f32[256,128]{1,0:T(8,128)} %momentum_ref.1) | copy-start | bytes 393220
  7.6 30.0 %copy-start.5 = (s32[8192]{0:T(1024)S(1)}, s32[8192]{0:T(1024)}, u32[]{:S(2)}) copy-start(s32[8192]{0:T(1024)} %param.12) | copy-start | bytes 98308
  7.6 8.1 %collective-permute-start.2 = (bf16[640,128]{1,0:T(8,128)(2,1)S(1)}, bf16[640,128]{1,0:T(8,128)(2,1)S(1)}, u32[]{:S(2)}, u32[]{:S(2)}) collective-permute-start(bf16[640,128]{1,0:T(8,128)(2,1)S(1)} %get-tuple-element.18), channel_id=1, source_target_pairs={{0,2},{1,3},{2,0},{3,1},{4,6},{5,7},{6,4},{7,5},{8,10},{9,11},{10,... | collective-permute-start | bytes 491528 | tf_op jit(solution)/shard_map/ppermute | solution.py:492
  12.0 8.5 %collective-permute-start.6 = (bf16[384,128]{1,0:T(8,128)(2,1)S(1)}, bf16[384,128]{1,0:T(8,128)(2,1)S(1)}, u32[]{:S(2)}, u32[]{:S(2)}) collective-permute-start(bf16[384,128]{1,0:T(8,128)(2,1)S(1)} %get-tuple-element.22), channel_id=1, source_target_pairs={{0,2},{1,3},{2,0},{3,1},{4,6},{5,7},{6,4},{7,5},{8,10},{9,11},{10,... | collective-permute-start | bytes 294920 | tf_op jit(solution)/shard_map/ppermute | solution.py:492
  12.1 16.4 %collective-permute-start.1 = (bf16[640,128]{1,0:T(8,128)(2,1)S(1)}, bf16[640,128]{1,0:T(8,128)(2,1)S(1)}, u32[]{:S(2)}, u32[]{:S(2)}) collective-permute-start(bf16[640,128]{1,0:T(8,128)(2,1)S(1)} %get-tuple-element.17), channel_id=1, source_target_pairs={{0,2},{1,3},{2,0},{3,1},{4,6},{5,7},{6,4},{7,5},{8,10},{9,11},{10,... | collective-permute-start | bytes 491528 | tf_op jit(solution)/shard_map/ppermute | solution.py:492
  15.8 12.7 %collective-permute-start.3 = (bf16[640,128]{1,0:T(8,128)(2,1)S(1)}, bf16[640,128]{1,0:T(8,128)(2,1)S(1)}, u32[]{:S(2)}, u32[]{:S(2)}) collective-permute-start(bf16[640,128]{1,0:T(8,128)(2,1)S(1)} %add_pieces.2), channel_id=1, source_target_pairs={{0,4},{1,5},{2,6},{3,7},{4,0},{5,1},{6,2},{7,3},{8,12},{9,13},{10,... | collective-permute-start | bytes 491528 | tf_op jit(solution)/shard_map/ppermute | solution.py:492
  18.9 9.6 %collective-permute-start.5 = (bf16[384,128]{1,0:T(8,128)(2,1)S(1)}, bf16[384,128]{1,0:T(8,128)(2,1)S(1)}, u32[]{:S(2)}, u32[]{:S(2)}) collective-permute-start(bf16[384,128]{1,0:T(8,128)(2,1)S(1)} %get-tuple-element.21), channel_id=1, source_target_pairs={{0,2},{1,3},{2,0},{3,1},{4,6},{5,7},{6,4},{7,5},{8,10},{9,11},{10,... | collective-permute-start | bytes 294920 | tf_op jit(solution)/shard_map/ppermute | solution.py:492
  20.5 8.0 %collective-permute-start.7 = (bf16[384,128]{1,0:T(8,128)(2,1)S(1)}, bf16[384,128]{1,0:T(8,128)(2,1)S(1)}, u32[]{:S(2)}, u32[]{:S(2)}) collective-permute-start(bf16[384,128]{1,0:T(8,128)(2,1)S(1)} %add_pieces.3), channel_id=1, source_target_pairs={{0,4},{1,5},{2,6},{3,7},{4,0},{5,1},{6,2},{7,3},{8,12},{9,13},{10,... | collective-permute-start | bytes 294920 | tf_op jit(solution)/shard_map/ppermute | solution.py:492
  29.2 4.6 %collective-permute-start.8 = (bf16[256,128]{1,0:T(8,128)(2,1)S(1)}, bf16[256,128]{1,0:T(8,128)(2,1)S(1)}, u32[]{:S(2)}, u32[]{:S(2)}) collective-permute-start(bf16[256,128]{1,0:T(8,128)(2,1)S(1)} %get-tuple-element.25), channel_id=1, source_target_pairs={{0,8},{1,9},{2,10},{3,11},{4,12},{5,13},{6,14},{7,15},{8,0},{9,1},... | collective-permute-start | bytes 196616 | tf_op jit(solution)/shard_map/ppermute | solution.py:492
  31.0 4.8 %collective-permute-start.9 = (bf16[256,128]{1,0:T(8,128)(2,1)S(1)}, bf16[256,128]{1,0:T(8,128)(2,1)S(1)}, u32[]{:S(2)}, u32[]{:S(2)}) collective-permute-start(bf16[256,128]{1,0:T(8,128)(2,1)S(1)} %get-tuple-element.26), channel_id=1, source_target_pairs={{0,16},{1,17},{2,18},{3,19},{4,20},{5,21},{6,22},{7,23},{8,24},{9,... | collective-permute-start | bytes 196616 | tf_op jit(solution)/shard_map/ppermute | solution.py:492
  32.5 5.2 %collective-permute-start.10 = (bf16[256,128]{1,0:T(8,128)(2,1)S(1)}, bf16[256,128]{1,0:T(8,128)(2,1)S(1)}, u32[]{:S(2)}, u32[]{:S(2)}) collective-permute-start(bf16[256,128]{1,0:T(8,128)(2,1)S(1)} %get-tuple-element.27), channel_id=1, source_target_pairs={{0,24},{1,25},{2,26},{3,27},{4,28},{5,29},{6,30},{7,31},{8,16},{9,... | collective-permute-start | bytes 196616 | tf_op jit(solution)/shard_map/ppermute | solution.py:492
  38.9 1.3 %collective-permute-start.11 = (bf16[256,128]{1,0:T(8,128)(2,1)S(1)}, bf16[256,128]{1,0:T(8,128)(2,1)S(1)}, u32[]{:S(2)}, u32[]{:S(2)}) collective-permute-start(bf16[256,128]{1,0:T(8,128)(2,1)S(1)} %get-tuple-element.29.ours_ref), channel_id=1, source_target_pairs={{0,1},{1,0},{2,3},{3,2},{4,5},{5,4},{6,7},{7,6},{8,9},{9,8},{10,11... | collective-permute-start | bytes 196616 | tf_op jit(solution)/shard_map/ppermute | solution.py:492
  40.3 3.3 %collective-permute-start.13 = (bf16[8,8192]{1,0:T(8,128)(2,1)S(1)}, bf16[8,8192]{1,0:T(8,128)(2,1)S(1)}, u32[]{:S(2)}, u32[]{:S(2)}) collective-permute-start(bf16[8,8192]{1,0:T(8,128)(2,1)S(1)} %chip_slab.1.own_ref), channel_id=1, source_target_pairs={{1,7},{3,5},{5,3},{7,1},{9,15},{11,13},{13,11},{15,9},{17,23},{19,... | collective-permute-start | bytes 393224 | tf_op jit(solution)/shard_map/ppermute | solution.py:492
  41.0 5.6 %collective-permute-start.12 = (bf16[8,8192]{1,0:T(8,128)(2,1)S(1)}, bf16[8,8192]{1,0:T(8,128)(2,1)S(1)}, u32[]{:S(2)}, u32[]{:S(2)}) collective-permute-start(bf16[8,8192]{1,0:T(8,128)(2,1)S(1)} %chip_slab.1.own_ref), channel_id=1, source_target_pairs={{0,2},{1,5},{2,0},{3,7},{4,6},{5,1},{6,4},{7,3},{8,10},{9,13},{10,... | collective-permute-start | bytes 393224 | tf_op jit(solution)/shard_map/ppermute | solution.py:492
  46.6 8.8 %collective-permute-start.19 = (bf16[16,8192]{1,0:T(8,128)(2,1)S(1)}, bf16[16,8192]{1,0:T(8,128)(2,1)S(1)}, u32[]{:S(2)}, u32[]{:S(2)}) collective-permute-start(bf16[16,8192]{1,0:T(8,128)(2,1)S(1)} %band_slab.1.refs_0_), channel_id=1, source_target_pairs={{0,24},{1,25},{2,26},{3,27},{4,28},{5,29},{6,30},{7,31},{8,16},{9,... | collective-permute-start | bytes 786440 | tf_op jit(solution)/shard_map/ppermute | solution.py:492
  47.2 12.4 %collective-permute-start.16 = (bf16[16,8192]{1,0:T(8,128)(2,1)S(1)}, bf16[16,8192]{1,0:T(8,128)(2,1)S(1)}, u32[]{:S(2)}, u32[]{:S(2)}) collective-permute-start(bf16[16,8192]{1,0:T(8,128)(2,1)S(1)} %band_slab.1.refs_0_), channel_id=1, source_target_pairs={{0,8},{1,9},{2,10},{3,11},{4,12},{5,13},{6,14},{7,15},{8,0},{9,1},... | collective-permute-start | bytes 786440 | tf_op jit(solution)/shard_map/ppermute | solution.py:492
  48.7 12.6 %collective-permute-start.14 = (bf16[16,8192]{1,0:T(8,128)(2,1)S(1)}, bf16[16,8192]{1,0:T(8,128)(2,1)S(1)}, u32[]{:S(2)}, u32[]{:S(2)}) collective-permute-start(bf16[16,8192]{1,0:T(8,128)(2,1)S(1)} %band_slab.1.refs_0_), channel_id=1, source_target_pairs={{0,16},{1,17},{2,18},{3,19},{4,20},{5,21},{6,22},{7,23},{8,24},{9,... | collective-permute-start | bytes 786440 | tf_op jit(solution)/shard_map/ppermute | solution.py:492
  50.2 12.0 %collective-permute-start.18 = (bf16[16,8192]{1,0:T(8,128)(2,1)S(1)}, bf16[16,8192]{1,0:T(8,128)(2,1)S(1)}, u32[]{:S(2)}, u32[]{:S(2)}) collective-permute-start(bf16[16,8192]{1,0:T(8,128)(2,1)S(1)} %band_slab.1.refs_0_), channel_id=1, source_target_pairs={{0,1},{1,0},{2,3},{3,2},{4,5},{5,4},{6,7},{7,6},{8,9},{9,8},{10,11... | collective-permute-start | bytes 786440 | tf_op jit(solution)/shard_map/ppermute | solution.py:492
  55.5 6.7 %collective-permute-start.20 = (bf16[16,8192]{1,0:T(8,128)(2,1)S(1)}, bf16[16,8192]{1,0:T(8,128)(2,1)S(1)}, u32[]{:S(2)}, u32[]{:S(2)}) collective-permute-start(bf16[16,8192]{1,0:T(8,128)(2,1)S(1)} %collective-permute-done.19.refs_2_), channel_id=1, source_target_pairs={{0,1},{1,0},{2,3},{3,2},{4,5},{5,4},{6,7},{7,6},{8,9},{9,8},{10,11... | collective-permute-start | bytes 786440 | tf_op jit(solution)/shard_map/ppermute | solution.py:492
  59.5 3.7 %collective-permute-start.17 = (bf16[16,8192]{1,0:T(8,128)(2,1)S(1)}, bf16[16,8192]{1,0:T(8,128)(2,1)S(1)}, u32[]{:S(2)}, u32[]{:S(2)}) collective-permute-start(bf16[16,8192]{1,0:T(8,128)(2,1)S(1)} %collective-permute-done.16.refs_2_), channel_id=1, source_target_pairs={{0,1},{1,0},{2,3},{3,2},{4,5},{5,4},{6,7},{7,6},{8,9},{9,8},{10,11... | collective-permute-start | bytes 786440 | tf_op jit(solution)/shard_map/ppermute | solution.py:492
  61.3 2.1 %collective-permute-start.15 = (bf16[16,8192]{1,0:T(8,128)(2,1)S(1)}, bf16[16,8192]{1,0:T(8,128)(2,1)S(1)}, u32[]{:S(2)}, u32[]{:S(2)}) collective-permute-start(bf16[16,8192]{1,0:T(8,128)(2,1)S(1)} %collective-permute-done.14.refs_0_), channel_id=1, source_target_pairs={{0,1},{1,0},{2,3},{3,2},{4,5},{5,4},{6,7},{7,6},{8,9},{9,8},{10,11... | collective-permute-start | bytes 786440 | tf_op jit(solution)/shard_map/ppermute | solution.py:492
